TPU v7x, 256 devices: a whole 4x4x8 slice. The times are simulated.
256 devices in a mesh: dp: 128 (over z, x, y), grp: 2 (over core).
Axes of the slice: x: 4, y: 4, z: 8, core: 2. Of those that a mesh axis runs over, the one named last changes fastest.
Arguments:
- embeds: bfloat16 [65536, 1024], P(('dp', 'grp')), may hold values from -7 to 7
- quality: float32 [65536], P(('dp', 'grp')), may hold values from 0.5 to 2
- domain_ids: int32 [65536], P(('dp', 'grp')), may hold values from 0 to 15, as said below
- domain_weight: float32 [16], replicated, may hold values from 0.5 to 2
- dest: int32 [65536], P(('dp', 'grp')), may hold values from 0 to 255, as said below
- counts: int32 [256], P(('dp', 'grp')), may hold values from 192 to 256, as said below
- winners: int32 [4], replicated, may hold values from 0 to 65535, as said below
Outputs:
- relaid: bfloat16 [131072, 1024], P(('dp', 'grp'))
- residual_gain: float32 [131072], P(('dp', 'grp'))
- chol_rows: float32 [4, 131072], P(None, ('dp', 'grp'))
Inputs may be any that keep to these rules, and one draw needn't show every extreme that they name: Rows 0 to counts - 1 of a device are valid, and one device has 256 valid rows. `dest`: destination device over dp and grp (index over dp+grp); among the valid rows of one device at most 2 name any one destination, and on every device some destination is named by exactly 2 valid rows. `domain_ids`: non-decreasing within each device's rows; a device's rows carry one domain number or two consecutive ones. `winners`: distinct valid rows, on distinct devices.
All inputs are finite; a program needn't handle non-finite values.
Results may differ from a plain program's by a relative error of at most 0.0048.
The roundings to bfloat16 on the way count: a program that leaves them out, or rounds other values in their place, can miss the bound.
Values may be sent and summed in bfloat16 or wider, within the bound.
No kernel may reach another device: no remote copies, remote signals or barrier semaphores. Data moves between devices by JAX's collectives and lax.ppermute only.
A program may use at most 64 MiB of HBM per device.

v0:
```python
import jax
import jax.numpy as jnp
from jax import lax
from jax.sharding import Mesh
from jax.sharding import PartitionSpec as P

DP_GRP = ("dp_0", "dp_1", "dp_2", "grp")
DP = ("dp_0", "dp_1", "dp_2")


RIDGE = 0.1


def sent_to_all(x, axis):
    count = lax.axis_size(axis)
    return lax.all_to_all(jnp.broadcast_to(x[None], (count, *x.shape)), axis, 0, 0, tiled=True)


def over_copies(x, axis):
    return sent_to_all(x, axis).sum(axis=0)


def over_axes(x, axes):
    far, near = axes
    nearer = over_copies(x, near)
    return over_copies(nearer, far)


def packed_total(arrays, axis):
    ends = [0]
    for a in arrays:
        ends.append(ends[-1] + a.size)
    subtotal = over_axes(jnp.concatenate([a.ravel() for a in arrays]), axis)
    return tuple((subtotal[b:e].reshape(a.shape) for a, b, e in zip(arrays, ends, ends[1:])))


def sent_together(arrays, axis, split_dim, concat_dim, along):
    columns = [a.reshape(*a.shape[:along], -1) for a in arrays]
    both = jnp.concatenate(columns, axis=along)
    out, at, done = (
        lax.all_to_all(both, axis, split_axis=split_dim, concat_axis=concat_dim, tiled=True),
        0,
        [],
    )
    for a, column in zip(arrays, columns):
        section = out[..., at : at + column.shape[along]]
        done.append(section.reshape(*section.shape[:along], *a.shape[along:]))
        at += column.shape[along]
    return tuple(done)


def body(embeds, quality, domain_ids, domain_weight, dest, counts, winners):
    shards = lax.axis_size(DP_GRP)
    pair_size = lax.axis_size("grp")
    spread_size = lax.axis_size(DP)
    slot_count = embeds.shape[0]
    feature_width = embeds.shape[1]
    step_count = winners.shape[0]
    domains = domain_weight.shape[0]
    per_pair = 2 * slot_count // shards
    balanced = shards * per_pair
    source = lax.axis_index(DP_GRP)
    row_index = jnp.arange(slot_count, dtype=jnp.int32)
    is_valid = row_index < counts[0]
    matches = domain_ids[:, None] == jnp.arange(domains, dtype=jnp.int32)[None, :]
    weight_row = jnp.sum(jnp.where(matches, domain_weight[None, :], 0.0), axis=1)
    row_quality = jnp.where(is_valid, quality * weight_row, 0.0).astype(jnp.bfloat16)
    targets = jnp.arange(shards, dtype=jnp.int32)
    dest_hot = ((dest[:, None] == targets[None, :]) & is_valid[:, None]).astype(jnp.bfloat16)
    strictly_lower = (row_index[None, :] < row_index[:, None]).astype(jnp.bfloat16)
    earlier_count = jnp.dot(strictly_lower, dest_hot, preferred_element_type=jnp.float32)
    dest_rank = jnp.sum(jnp.where(dest_hot > 0, earlier_count, 0.0), axis=1).astype(jnp.int32)
    send_slot = jnp.where(is_valid, dest * per_pair + dest_rank, balanced)
    bal_place = (dest * balanced + source * per_pair + dest_rank).astype(jnp.float32)
    send_rows = (
        jnp.zeros((balanced, feature_width), jnp.bfloat16).at[send_slot].set(embeds, mode="drop")
    )
    send_rows = send_rows.reshape(spread_size, pair_size, per_pair, feature_width)
    send_quality = jnp.zeros((balanced,), jnp.bfloat16).at[send_slot].set(row_quality, mode="drop")
    send_quality = send_quality.reshape(spread_size, pair_size, per_pair)
    quality_wide = row_quality.astype(jnp.float32)
    chosen = row_index[None, :] == (winners - source * slot_count)[:, None]
    picked_rows = jnp.dot(chosen.astype(jnp.bfloat16), embeds, preferred_element_type=jnp.float32)
    picked_quality = jnp.sum(jnp.where(chosen, quality_wide[None, :], 0.0), axis=1)
    picked_place = jnp.sum(jnp.where(chosen, bal_place[None, :], 0.0), axis=1)
    win_rows, win_quality, win_place = packed_total(
        (picked_rows, picked_quality, picked_place), (("dp_0", "dp_1"), ("dp_2", "grp"))
    )
    win_short = win_rows.astype(jnp.bfloat16)
    first_hop = sent_together((send_rows, send_quality), DP, 0, 0, 3)
    rows_in = lax.all_to_all(first_hop[0], "grp", split_axis=1, concat_axis=1, tiled=True)
    quality_in = lax.all_to_all(first_hop[1], "grp", split_axis=1, concat_axis=1, tiled=True)
    row_norms = jnp.einsum("abmd,abmd->abm", rows_in, rows_in, preferred_element_type=jnp.float32)
    kernel_dots = jnp.einsum(
        "abmd,kd->abmk", rows_in, win_short, preferred_element_type=jnp.float32
    )
    arrived = (rows_in, quality_in, row_norms, kernel_dots)
    relaid = arrived[0].reshape(balanced, feature_width)
    bal_quality = arrived[1].reshape(balanced).astype(jnp.float32)
    row_norms = arrived[2].reshape(balanced)
    residual_gain = jnp.where(
        bal_quality > 0, bal_quality * bal_quality * row_norms / feature_width + RIDGE, 0.0
    )
    local_place = (source * balanced + jnp.arange(balanced, dtype=jnp.int32)).astype(jnp.float32)
    dots_all = arrived[3].reshape(balanced, step_count)
    kept_rows = []
    kept_quality = []
    kept_columns = []
    kept_roots = []
    chol_list = []
    for turn_index in range(step_count):
        row_now = win_short[turn_index]
        quality_now = win_quality[turn_index]
        place_now = win_place[turn_index]
        dot_now = dots_all[:, turn_index]
        column_now = []
        for prior_step in range(turn_index):
            cross_term = (
                kept_quality[prior_step]
                * quality_now
                * jnp.dot(kept_rows[prior_step], row_now, preferred_element_type=jnp.float32)
                / feature_width
            )
            for earlier in range(prior_step):
                cross_term = cross_term - kept_columns[prior_step][earlier] * column_now[earlier]
            column_now.append(cross_term / kept_roots[prior_step])
        self_term = (
            quality_now
            * quality_now
            * jnp.dot(row_now, row_now, preferred_element_type=jnp.float32)
            / feature_width
            + RIDGE
        )
        for prior_step in range(turn_index):
            self_term = self_term - column_now[prior_step] * column_now[prior_step]
        root_now = jnp.sqrt(self_term)
        inner_sum = jnp.zeros_like(residual_gain)
        for prior_step in range(turn_index):
            inner_sum = inner_sum + chol_list[prior_step] * column_now[prior_step]
        ridge_hit = jnp.where(local_place == place_now, RIDGE, 0.0)
        new_entry = (
            bal_quality * quality_now * dot_now / feature_width + ridge_hit - inner_sum
        ) / root_now
        chol_list.append(new_entry)
        residual_gain = residual_gain - new_entry * new_entry
        kept_rows.append(row_now)
        kept_quality.append(quality_now)
        kept_columns.append(column_now)
        kept_roots.append(root_now)
    return (relaid, residual_gain, jnp.stack(chol_list))


def solution(mesh):
    finer = Mesh(mesh.devices.reshape(8, 4, 4, mesh.shape["grp"]), ("dp_0", "dp_1", "dp_2", "grp"))
    placed = (P(DP_GRP, None), P(DP_GRP), P(DP_GRP), P(), P(DP_GRP), P(DP_GRP), P())
    return jax.shard_map(
        body,
        mesh=finer,
        in_specs=placed,
        out_specs=(P(DP_GRP, None), P(DP_GRP), P(None, DP_GRP)),
        check_vma=False,
    )
```

profile of v0, /device:TPU:1, one launch (start us, length us, event | category | flops | bytes accessed | tf_op | source)
XLA Modules:
  0.0 111.5 jit_solution(16072161169411447763)
XLA Ops:
  1.3 0.7 broadcast_subtract_fusion
  2.0 1.3 %convolution_bitcast_fusion = f32[1,8,4,128]{3,2,1,0:T(4,128)S(1)} fusion(bf16[256,1024]{1,0:T(8,128)(2,1)} %param.7, s32[4]{0:T(128)S(1)} %broadcast_subtract_fusion), kind=kOutput, calls=%fused_computation.7 | convolution fusion | flops 2098176 | bytes 540688 | tf_op jit(solution)/shard_map/dot_general | solution.py:83
  3.3 1.0 fusion.1
  4.8 11.0 %all_to_all.27 = f32[8,1,4104]{2,1,0:T(1,128)S(1)} all-to-all(f32[8,1,4104]{2,1,0:T(1,128)S(1)} %broadcast_in_dim.99), channel_id=1, replica_groups=mesh['dp_0'=8,'dp_1'=4,'dp_2'=4,'grp'=2] {'dp_2','grp'}, dimensions={0} | all-to-all | bytes 262656 | tf_op jit(solution)/shard_map/all_to_all | solution.py:16
  15.9 1.1 broadcast_in_dim.100
  17.0 11.0 %all-to-all-start.4 = ((f32[32,1,4104]{2,1,0:T(1,128)}), f32[32,1,4104]{2,1,0:T(1,128)S(1)}, u32[]{:S(2)}, u32[]{:S(2)}) async-start(f32[32,1,4104]{2,1,0:T(1,128)} %broadcast_in_dim.100), calls=%async_computation.4 | async-start | bytes 1081344 | tf_op jit(solution)/shard_map/all_to_all | solution.py:16
  28.0 2.4 %scatter_custom_fusion = bf16[512,1024]{1,0:T(8,128)(2,1)S(1)} fusion(s32[256]{0:T(256)S(1)} %get-tuple-element.34, bf16[256,1024]{1,0:T(8,128)(2,1)} %param.7, bf16[]{:T(256)} %constant.44.clone.1), kind=kCustom, calls=%fused_computation.8 | custom fusion | bytes 1049088 | tf_op jit(solution)/shard_map/scatter | solution.py:76
  30.5 2.2 %scatter_custom_fusion.1 = bf16[512]{0:T(512)(128)(2,1)S(1)} fusion(s32[256]{0:T(256)S(1)} %get-tuple-element.34, bf16[256]{0:T(256)(128)(2,1)S(1)} %get-tuple-element.20, bf16[]{:T(256)} %constant.44.clone.1), kind=kCustom, calls=%fused_computation.90 | custom fusion | bytes 1026 | tf_op jit(solution)/shard_map/scatter | solution.py:79
  32.6 0.3 reshape_reshape.4
  32.9 0.4 reshape.292
  33.3 2.1 %pad_maximum_fusion = bf16[128,2,2,1025]{3,2,1,0:T(2,128)(2,1)} fusion(bf16[128,2,2,1]{3,2,1,0:T(2,128)(2,1)S(1)} %reshape_reshape.4, bf16[128,2,2,1024]{3,2,1,0:T(2,128)(2,1)S(1)} %reshape.292), kind=kLoop, calls=%fused_computation.4 | loop fusion | flops 2099200 | bytes 2099200 | tf_op jit(solution)/shard_map/concatenate | solution.py:39
  35.5 8.4 %all-to-all-done.4 = f32[32,1,4104]{2,1,0:T(1,128)S(1)} async-done(((f32[32,1,4104]{2,1,0:T(1,128)}), f32[32,1,4104]{2,1,0:T(1,128)S(1)}, u32[]{:S(2)}, u32[]{:S(2)}) %all-to-all-start.4) | async-done | bytes 525344 | tf_op jit(solution)/shard_map/all_to_all | solution.py:16
  43.9 8.4 %all-to-all-start = ((bf16[128,2,2,1025]{3,2,1,0:T(2,128)(2,1)}), bf16[128,2,2,1025]{3,2,1,0:T(2,128)(2,1)S(1)}, u32[]{:S(2)}, u32[]{:S(2)}) async-start(bf16[128,2,2,1025]{3,2,1,0:T(2,128)(2,1)} %pad_maximum_fusion), calls=%async_computation | async-start | bytes 2359296 | tf_op jit(solution)/shard_map/all_to_all | solution.py:41
  52.4 0.3 reduce_sum.59
  52.7 0.7 fusion.46
  65.9 0.7 fusion.11
  73.3 9.6 %all-to-all-done = bf16[128,2,2,1025]{3,2,1,0:T(2,128)(2,1)S(1)} async-done(((bf16[128,2,2,1025]{3,2,1,0:T(2,128)(2,1)}), bf16[128,2,2,1025]{3,2,1,0:T(2,128)(2,1)S(1)}, u32[]{:S(2)}, u32[]{:S(2)}) %all-to-all-start) | async-done | bytes 1049632 | tf_op jit(solution)/shard_map/all_to_all | solution.py:41
  82.9 0.7 copy.64
  83.6 0.7 slice.90
  84.3 0.7 copy.62
  85.0 8.7 %all_to_all.28 = bf16[128,2,2,1024]{3,2,0,1:T(2,128)(2,1)S(1)} all-to-all(bf16[128,2,2,1024]{3,2,0,1:T(2,128)(2,1)S(1)} %copy.62), channel_id=1, replica_groups=mesh['dp_0'=8,'dp_1'=4,'dp_2'=4,'grp'=2] {'grp'}, dimensions={1} | all-to-all | bytes 2097152 | tf_op jit(solution)/shard_map/all_to_all | solution.py:91
  93.7 3.6 %all-to-all-start.2 = ((bf16[128,2,2]{0,2,1:T(2,128)(2,1)}), bf16[128,2,2]{0,2,1:T(2,128)(2,1)S(1)}, u32[]{:S(2)}, u32[]{:S(2)}) async-start(bf16[128,2,2]{0,2,1:T(2,128)(2,1)} %bitcast.1), calls=%async_computation.2 | async-start | bytes 2048 | tf_op jit(solution)/shard_map/all_to_all | solution.py:92
  97.3 1.2 %fusion = f32[128,2,2]{2,0,1:T(8,128)S(1)} fusion(bf16[128,2,2,1024]{3,2,0,1:T(2,128)(2,1)S(1)} %all_to_all.28), kind=kLoop, calls=%fused_computation.3 | loop fusion | flops 1572352 | bytes 1050624
  98.5 2.5 %convert_multiply_fusion.14 = (f32[128,2,2]{0,2,1:T(2,128)S(1)}, f32[128,2,2]{0,2,1:T(2,128)S(1)}, f32[128,2,2]{0,2,1:T(2,128)S(1)}, f32[128,2,2]{0,2,1:T(2,128)S(1)}, f32[128,2,2]{0,2,1:T(2,128)S(1)}) fusion(bf16[128,2,2]{0,2,1:T(2,128)(2,1)S(1)} %all-to-all-done.2, f32[]{:T(128)} %bitcast.2, f32[]{:T(128)} %bitcast.5, f32[]{:T(128)} %bitcast.8, ...), kind=kLoop, calls=%fused_computation.38 | loop fusion | flops 5632 | bytes 13328 | tf_op jit(solution)/shard_map/mul | solution.py:142
  101.7 0.2 mul.506
  102.8 0.2 mul.516
  103.2 0.7 copy.63
  103.9 0.4 reshape.293
  104.4 0.4 fusion.48
  105.2 2.6 %fusion.39 = (f32[1,512]{1,0:T(1,128)S(1)}, f32[1,512]{1,0:T(1,128)S(1)}, f32[1,512]{1,0:T(1,128)S(1)}, f32[1,512]{1,0:T(1,128)S(1)}) fusion(f32[1,512]{1,0:T(1,128)S(1)} %mul.516, f32[]{:T(128)S(6)} %sqrt.15, f32[]{:T(128)S(6)} %div.191, f32[]{:T(128)S(6)} %div.189, f32[]{:T(128)S(6)} %div.187, f32[]{:T(128)} %bitcast.13, s32[]{:T(128)S(6)} %mul.445, ...), kind=kLoop, calls=%fused_computation.86 | loop fusion | flops 19456 | bytes 24636 | tf_op jit(solution)/shard_map/div | solution.py:141
  107.7 0.6 pad_maximum_fusion.1
  108.3 3.1 %fusion.20 = f32[512]{0:T(512)} fusion(f32[512]{0:T(512)S(1)} %mul.481, f32[512]{0:T(512)S(1)} %bitcast.64, f32[512]{0:T(512)S(1)} %mul.463, f32[512]{0:T(512)S(1)} %bitcast.65, f32[512]{0:T(512)S(1)} %mul.451, f32[512]{0:T(512)S(1)} %bitcast.66, f32[512]{0:T(512)S(1)} %reshape.299, f32[512]{0:T(512)S(1)} %mul.443, f32[512]{0:T(512)S(1)} %bitcast.63, ...), kind=kLoop, calls=%fused_computation.57 | loop fusion | flops 23552 | bytes 20540 | tf_op jit(solution)/shard_map/sub | solution.py:145
  (37 shorter events, 2.9 us)
Async XLA Ops:
  0.6 3.8 %copy-start.1 = (s32[256]{0:T(256)S(1)}, s32[256]{0:T(256)}, u32[]{:S(2)}) copy-start(s32[256]{0:T(256)} %param.11) | copy-start | bytes 3076
  0.6 3.6 %copy-start.4 = (f32[16]{0:T(128)S(1)}, f32[16]{0:T(128)}, u32[]{:S(2)}) copy-start(f32[16]{0:T(128)} %param.10) | copy-start | bytes 196
  0.7 3.6 %copy-start.2 = (s32[256]{0:T(256)S(1)}, s32[256]{0:T(256)}, u32[]{:S(2)}) copy-start(s32[256]{0:T(256)} %param.9) | copy-start | bytes 3076
  0.7 3.8 %copy-start.3 = (f32[256]{0:T(256)S(1)}, f32[256]{0:T(256)}, u32[]{:S(2)}) copy-start(f32[256]{0:T(256)} %param.8) | copy-start | bytes 3076
  17.0 26.9 %all-to-all-start.4 = ((f32[32,1,4104]{2,1,0:T(1,128)}), f32[32,1,4104]{2,1,0:T(1,128)S(1)}, u32[]{:S(2)}, u32[]{:S(2)}) async-start(f32[32,1,4104]{2,1,0:T(1,128)} %broadcast_in_dim.100), calls=%async_computation.4 | async-start | bytes 1081344 | tf_op jit(solution)/shard_map/all_to_all | solution.py:16
  43.9 38.9 %all-to-all-start = ((bf16[128,2,2,1025]{3,2,1,0:T(2,128)(2,1)}), bf16[128,2,2,1025]{3,2,1,0:T(2,128)(2,1)S(1)}, u32[]{:S(2)}, u32[]{:S(2)}) async-start(bf16[128,2,2,1025]{3,2,1,0:T(2,128)(2,1)} %pad_maximum_fusion), calls=%async_computation | async-start | bytes 2359296 | tf_op jit(solution)/shard_map/all_to_all | solution.py:41
  93.7 4.8 %all-to-all-start.2 = ((bf16[128,2,2]{0,2,1:T(2,128)(2,1)}), bf16[128,2,2]{0,2,1:T(2,128)(2,1)S(1)}, u32[]{:S(2)}, u32[]{:S(2)}) async-start(bf16[128,2,2]{0,2,1:T(2,128)(2,1)} %bitcast.1), calls=%async_computation.2 | async-start | bytes 2048 | tf_op jit(solution)/shard_map/all_to_all | solution.py:92
  104.4 7.1 %copy-start = (bf16[512,1024]{1,0:T(8,128)(2,1)}, bf16[512,1024]{1,0:T(8,128)(2,1)S(1)}, u32[]{:S(2)}) copy-start(bf16[512,1024]{1,0:T(8,128)(2,1)S(1)} %reshape.293) | copy-start | bytes 3145732
where the time goes:
time: 112 us; the launch traced here: 111 us
  starting transfers between devices  23 us (21%)
  between operations  20.7 us (18%)
  blocking collectives  19.7 us (18%)
  waiting for transfers between devices  18 us (16%)
  other arithmetic  14.2 us (13%)
  local copies, waits for them, and re-layouts  13.2 us (12%)
  matrix products  2.65 us (2%)
    all_to_all x1, blocking collectives, sent_to_all(): lax.all_to_all(jnp.broadcast_to(x[None], (count, *x.shape)), axis, 0, 0,...  11 us
    all_to_all x1, starting transfers between devices, sent_to_all(): lax.all_to_all(jnp.broadcast_to(x[None], (count, *x.shape)), axis, 0, 0,...  11 us
    all_to_all x1, waiting for transfers between devices, sent_together(): lax.all_to_all(both, axis, split_axis=split_dim, concat_axis=concat_dim,...  9.56 us
    all_to_all x1, blocking collectives, body(): lax.all_to_all(first_hop[0], 'grp', split_axis=1, concat_axis=1, tiled=True)  8.7 us
    all_to_all x1, waiting for transfers between devices, sent_to_all(): lax.all_to_all(jnp.broadcast_to(x[None], (count, *x.shape)), axis, 0, 0,...  8.45 us
    all_to_all x1, starting transfers between devices, sent_together(): lax.all_to_all(both, axis, split_axis=split_dim, concat_axis=concat_dim,...  8.42 us
    all_to_all x1, starting transfers between devices, body(): lax.all_to_all(first_hop[1], 'grp', split_axis=1, concat_axis=1, tiled=True)  3.56 us
    sub x1, other arithmetic, body(): residual_gain = residual_gain - new_entry * new_entry  3.13 us
  transfers between devices with their start and end apart: 3, of which 2 were waited for; matrix products, arithmetic and copies ran while one was open for 9% of the time, Pallas kernels for 0%

commit v1 on v0

v1 whole, which is shorter than its diff:
```python
import jax
import jax.numpy as jnp
from jax import lax
from jax.experimental import pallas as pl
from jax.experimental.pallas import tpu as pltpu
from jax.sharding import Mesh
from jax.sharding import PartitionSpec as P

ALL = ("z", "x", "y", "core")
PLANE = ("x", "y", "core")
RING = ("x", "y", "core", "z")
RIDGE = 0.1
LANES = 128
F32 = jnp.float32
BF16 = jnp.bfloat16
VMEM = pl.BlockSpec(memory_space=pltpu.VMEM)
SMEM = pl.BlockSpec(memory_space=pltpu.SMEM)


def iota(shape, dim):
    return lax.broadcasted_iota(jnp.int32, shape, dim)


def prep(shards, plane, rel, counts, weight, emb, dest, quality, domain, slot_out, aux_out, picks):
    slots, width = emb.shape
    steps = rel.shape[0]
    square = (slots, slots)
    row, col = iota(square, 0), iota(square, 1)
    dest_row = dest[...].astype(F32)
    across = jnp.broadcast_to(dest_row, square)
    down = jnp.sum(jnp.where(row == col, across, 0.0), axis=1, keepdims=True)
    earlier = (down == across) & (row < col)
    rank = jnp.sum(jnp.where(earlier, 1.0, 0.0), axis=0, keepdims=True)
    lane = iota((1, slots), 1)
    valid = lane < counts[0]
    ring = shards // plane
    to = dest[...]
    to = lax.rem(to, plane) * ring + lax.div(to, plane)
    slot = jnp.where(valid, 2.0 * to.astype(F32) + rank, -1.0)
    slot_out[...] = slot.astype(jnp.int32)
    scale = jnp.zeros((1, slots), F32)
    for k in range(weight.shape[0]):
        scale = jnp.where(domain[...] == k, weight[k], scale)
    row_quality = (quality[...] * scale).astype(BF16).astype(F32)

    peer = (iota((shards, slots), 0) * 2).astype(F32)
    first = jnp.sum(jnp.where(slot == peer, row_quality, 0.0), axis=1, keepdims=True)
    second = jnp.sum(jnp.where(slot == peer + 1.0, row_quality, 0.0), axis=1, keepdims=True)

    turn = iota((8, slots), 0)
    wanted = jnp.full((8, slots), -1, jnp.int32)
    for t in range(steps):
        wanted = jnp.where(turn == t, rel[t], wanted)
    chosen = (iota((8, slots), 1) == wanted) & valid
    spread = jnp.zeros((8, LANES), F32)
    turn_out, lane_out = iota((8, LANES), 0), iota((8, LANES), 1)
    for k, value in enumerate((row_quality, dest_row, rank)):
        mine = jnp.sum(jnp.where(chosen, value, 0.0), axis=1, keepdims=True)
        here = (lane_out == turn_out + (2 + k * steps)) & (turn_out < steps)
        spread = spread + jnp.where(here, mine, 0.0)
    scalars = jnp.sum(spread, axis=0, keepdims=True)
    lanes = iota((shards, LANES), 1)
    side = jnp.where(lanes == 0, first, jnp.where(lanes == 1, second, scalars))

    picked = jnp.dot(chosen.astype(F32).astype(BF16), emb[...], preferred_element_type=F32)
    parts = width // LANES
    for t in range(steps):
        for j in range(parts):
            picks[t * parts + j : t * parts + j + 1, :] = picked[t : t + 1, j * LANES : (j + 1) * LANES]
    spot = iota((shards, plane), 0) - ring * iota((shards, plane), 1)
    share = ((spot >= 0) & (spot < ring)).astype(F32).astype(BF16)
    piece = jnp.dot(share, picks[...].astype(BF16), preferred_element_type=F32)
    aux_out[:, :LANES] = piece.astype(BF16)
    aux_out[:, LANES:] = side.astype(BF16)


def place_rows(slot, emb, out):
    rows = out.shape[0]
    slots = slot.shape[1]
    block = 128
    for at in range(0, rows, block):
        hot = (iota((block, slots), 0) + at) == slot[...]
        hot = hot.astype(F32).astype(BF16)
        out[at : at + block, :] = jnp.dot(hot, emb[...], preferred_element_type=F32).astype(BF16)


def select(ring, winners, base, rows, pieces, side, gain_out, chol_out, wide):
    balanced, width = rows.shape
    steps = chol_out.shape[0]
    shards = side.shape[0]
    parts = width // LANES
    wide[...] = jnp.zeros_like(wide)
    piece = pieces[...].astype(F32)
    for t in range(steps):
        for j in range(parts):
            wide[t : t + 1, j * LANES : (j + 1) * LANES] = piece[t * parts + j : t * parts + j + 1, :]
    win = wide[...].astype(BF16)
    nt = (((1,), (1,)), ((), ()))
    dots = lax.dot_general(win, rows[...], nt, preferred_element_type=F32)
    gram = lax.dot_general(win, win, nt, preferred_element_type=F32)
    partial = jnp.zeros((balanced, LANES), F32)
    for j in range(parts):
        x = rows[:, j * LANES : (j + 1) * LANES].astype(F32)
        partial = partial + x * x
    ones = jnp.ones((8, LANES), BF16)
    norms = jnp.zeros((8, balanced), F32)
    rest = partial
    for _ in range(3):
        part = rest.astype(BF16)
        rest = rest - part.astype(F32)
        norms = norms + lax.dot_general(ones, part, nt, preferred_element_type=F32)
    norms = norms[0:1, :]

    received = side[...].astype(F32)
    grid = (shards, balanced)
    source, slot = iota(grid, 0), iota(grid, 1)
    source = lax.rem(source, ring) * (shards // ring) + lax.div(source, ring)
    own = jnp.where(slot == 2 * source, received[:, 0:1], 0.0) + jnp.where(slot == 2 * source + 1, received[:, 1:2], 0.0)
    quality = jnp.sum(own, axis=0, keepdims=True)
    scalars = jnp.sum(received, axis=0, keepdims=True)
    win_quality = [scalars[:, 2 + t : 3 + t] for t in range(steps)]
    win_dest = [scalars[:, 2 + steps + t : 3 + steps + t].astype(jnp.int32) for t in range(steps)]
    win_rank = [scalars[:, 2 + 2 * steps + t : 3 + 2 * steps + t].astype(jnp.int32) for t in range(steps)]

    gain = jnp.where(quality > 0, quality * quality * norms / width + RIDGE, 0.0)
    local = iota((1, balanced), 1) + base[0]
    columns, roots, chol = [], [], []
    for t in range(steps):
        column = []
        for k in range(t):
            cross = win_quality[k] * win_quality[t] * gram[k : k + 1, t : t + 1] / width
            for e in range(k):
                cross = cross - columns[k][e] * column[e]
            column.append(cross / roots[k])
        own_gain = win_quality[t] * win_quality[t] * gram[t : t + 1, t : t + 1] / width + RIDGE
        for k in range(t):
            own_gain = own_gain - column[k] * column[k]
        root = jnp.sqrt(own_gain)
        inner = jnp.zeros((1, balanced), F32)
        for k in range(t):
            inner = inner + chol[k] * column[k]
        place = win_dest[t] * balanced + winners[t] // (balanced // 2) * 2 + win_rank[t]
        hit = jnp.where(local == place, RIDGE, 0.0)
        entry = (quality * win_quality[t] * dots[t : t + 1, :] / width + hit - inner) / root
        gain = gain - entry * entry
        columns.append(column)
        roots.append(root)
        chol.append(entry)
        chol_out[t : t + 1, :] = entry
    gain_out[...] = gain


def body(embeds, quality, domain_ids, domain_weight, dest, counts, winners):
    shards = lax.axis_size(ALL)
    plane = lax.axis_size(PLANE)
    slots, width = embeds.shape
    steps = winners.shape[0]
    balanced = 2 * slots
    ring = shards // plane
    me = lax.axis_index(ALL)

    slot, aux = pl.pallas_call(
        lambda *refs: prep(shards, plane, *refs),
        in_specs=[SMEM, SMEM, SMEM, VMEM, VMEM, VMEM, VMEM],
        out_specs=[VMEM, VMEM],
        out_shape=[
            jax.ShapeDtypeStruct((1, slots), jnp.int32),
            jax.ShapeDtypeStruct((shards, 2 * LANES), BF16),
        ],
        scratch_shapes=[pltpu.VMEM((plane, LANES), F32)],
        name="prep",
    )(
        winners - me * slots,
        counts,
        domain_weight,
        embeds,
        dest.reshape(1, slots),
        quality.reshape(1, slots),
        domain_ids.reshape(1, slots),
    )
    side_in = lax.all_to_all(aux.reshape(shards, 2, LANES), RING, 0, 0, tiled=True)
    send = pl.pallas_call(
        place_rows,
        in_specs=[VMEM, VMEM],
        out_specs=VMEM,
        out_shape=jax.ShapeDtypeStruct((balanced, width), BF16),
        name="place_rows",
        cost_estimate=pl.CostEstimate(flops=2 * balanced * slots * width, bytes_accessed=1 << 21, transcendentals=0),
    )(slot, embeds)
    rows_in = lax.all_to_all(send.reshape(shards, 2, width), RING, 0, 0, tiled=True)
    piece = jnp.sum(side_in[:, 0, :].astype(F32), axis=0).astype(BF16)
    pieces = lax.all_to_all(jnp.broadcast_to(piece[None, None], (plane, 1, LANES)), PLANE, 0, 0, tiled=True)
    relaid = rows_in.reshape(plane, ring, 2, width).swapaxes(0, 1).reshape(balanced, width)
    gain, chol = pl.pallas_call(
        lambda *refs: select(ring, *refs),
        in_specs=[SMEM, SMEM, VMEM, VMEM, VMEM],
        out_specs=[VMEM, VMEM],
        out_shape=[
            jax.ShapeDtypeStruct((1, balanced), F32),
            jax.ShapeDtypeStruct((steps, balanced), F32),
        ],
        scratch_shapes=[pltpu.VMEM((8, width), F32)],
        name="select",
    )(
        winners,
        (me * balanced).reshape(1),
        relaid,
        pieces.reshape(plane, LANES),
        side_in[:, 1, :],
    )
    return relaid, gain.reshape(balanced), chol


def solution(mesh):
    finer = Mesh(mesh.devices.reshape(8, 4, 4, mesh.shape["grp"]), ALL)
    placed = (P(ALL, None), P(ALL), P(ALL), P(), P(ALL), P(ALL), P())
    return jax.shard_map(
        body,
        mesh=finer,
        in_specs=placed,
        out_specs=(P(ALL, None), P(ALL), P(None, ALL)),
        check_vma=False,
    )
```

time: 112 us -> 90.5 us (0.81)
  between operations: 20.7 us -> 1.35 us
  waiting for transfers between devices: 18 us -> 33.3 us
  other arithmetic: 14.2 us -> 0.81 us
  starting transfers between devices: 23 us -> 10.4 us
  blocking collectives: 19.7 us -> 28.5 us
  Pallas kernels: 0 us -> 7.43 us
  local copies, waits for them, and re-layouts: 13.2 us -> 8.43 us
  matrix products: 2.65 us -> 0 us
    all_to_all x3 -> x2, waiting for transfers between devices: 18 us -> 33.3 us  [the longest x1 30.9 us: body(): lax.all_to_all(send.reshape(shards, 2, width), RING, 0, 0, tiled=True)]
    all_to_all x3 -> x2, starting transfers between devices: 23 us -> 10.4 us  [the longest x1 6.29 us: body(): lax.all_to_all(send.reshape(shards, 2, width), RING, 0, 0, tiled=True)]
    all_to_all x2 -> x1, blocking collectives: 19.7 us -> 28.5 us  [body(): lax.all_to_all(aux.reshape(shards, 2, LANES), RING, 0, 0, tiled=True)]
    pallas_call x0 -> x3, Pallas kernels: none -> 7.43 us  [the longest x1 2.88 us: body(): pl.pallas_call(lambda *refs: select(ring, *refs), in_specs=[SMEM, SMEM, V...]
    scatter x2 -> x0, local copies, waits for them, and re-layouts: 4.57 us -> none  [the longest x1 2.41 us: body(): jnp.zeros((balanced, feature_width), jnp.bfloat16).at[send_slot]]
    sub x2 -> x1, other arithmetic: 3.79 us -> 0.51 us  [body(): winners - me * slots]
    slice x7 -> x0, local copies, waits for them, and re-layouts: 2.92 us -> none  [the longest x4 2.21 us: sent_together(): section = out[..., at:at + column.shape[along]]]
    reshape x2 -> x3, local copies, waits for them, and re-layouts: 0.88 us -> 3.58 us  [the longest x1 2.24 us: body(): send.reshape(shards, 2, width)]
  transfers between devices with their start and end apart: 3 -> 2, of which waited for: 2 -> 2; matrix products, arithmetic and copies ran while one was open for 9% -> 4% of each run, Pallas kernels for 0% -> 3%
where the time goes in v1:
time: 90.5 us; the launch traced here: 90.2 us
  waiting for transfers between devices  33.3 us (37%)
  blocking collectives  28.5 us (31%)
  starting transfers between devices  10.4 us (11%)
  local copies, waits for them, and re-layouts  8.43 us (9%)
  Pallas kernels  7.43 us (8%)
  between operations  1.35 us (1%)
    all_to_all x1, waiting for transfers between devices, body(): lax.all_to_all(send.reshape(shards, 2, width), RING, 0, 0, tiled=True)  30.9 us
    all_to_all x1, blocking collectives, body(): lax.all_to_all(aux.reshape(shards, 2, LANES), RING, 0, 0, tiled=True)  28.5 us
    all_to_all x1, starting transfers between devices, body(): lax.all_to_all(send.reshape(shards, 2, width), RING, 0, 0, tiled=True)  6.29 us
    all_to_all x1, starting transfers between devices, body(): lax.all_to_all(jnp.broadcast_to(piece[None, None], (plane, 1, LANES)), PL...  4.08 us
    pallas_call x1, Pallas kernels, body(): pl.pallas_call(lambda *refs: select(ring, *refs), in_specs=[SMEM, SMEM, V...  2.88 us
    pallas_call x1, Pallas kernels, body(): pl.pallas_call(place_rows, in_specs=[VMEM, VMEM], out_specs=VMEM, out_sha...  2.48 us
    all_to_all x1, waiting for transfers between devices, body(): lax.all_to_all(jnp.broadcast_to(piece[None, None], (plane, 1, LANES)), PL...  2.36 us
    reshape x1, local copies, waits for them, and re-layouts, body(): send.reshape(shards, 2, width)  2.24 us
  transfers between devices with their start and end apart: 2, of which 2 were waited for; matrix products, arithmetic and copies ran while one was open for 4% of the time, Pallas kernels for 3%

profile of v1, /device:TPU:1, one launch (start us, length us, event | category | flops | bytes accessed | tf_op | source)
XLA Modules:
  0.0 90.2 jit_solution(8658509715290226382)
XLA Ops:
  1.3 0.0 copy-start
  1.3 0.6 copy-done
  1.9 0.5 broadcast_subtract_fusion.refs_0_
  2.5 2.1 %prep.1 = (s32[1,256]{1,0:T(1,128)}, bf16[256,256]{1,0:T(8,128)(2,1)}) custom-call(s32[4]{0:T(128)} %broadcast_subtract_fusion.refs_0_, s32[1]{0:T(128)S(6)} %copy.32.refs_1_, f32[16]{0:T(128)} %refs_2_.1, bf16[256,1024]{1,0:T(8,128)(2,1)} %emb.1, s32[1,256]{1,0:T(1,128)} %bitcast.21, f32[1,256]{1,0:T(1,128)} %bitcast.22, s32[1,256]{1,0:T(1,128)} %bitcast.23), custom_call_target="tpu_custom_call" | custom-call | tf_op jit(solution)/shard_map/prep/pallas_call | solution.py:162
  4.5 1.0 %copy.21 = bf16[256,256]{0,1:T(8,128)(2,1)S(1)} copy(bf16[256,256]{1,0:T(8,128)(2,1)} %get-tuple-element.8) | data formatting | bytes 262144 | tf_op jit(solution)/shard_map/prep/pallas_call | solution.py:162
  5.5 0.1 copy.22
  5.7 28.5 %all_to_all.15 = bf16[256,2,128]{2,1,0:T(2,128)(2,1)S(1)} all-to-all(bf16[256,2,128]{2,1,0:T(2,128)(2,1)S(1)} %copy.22), channel_id=1, replica_groups=mesh['z'=8,'x'=4,'y'=4,'core'=2] {'x','y','core','z'}, dimensions={0} | all-to-all | bytes 262144 | tf_op jit(solution)/shard_map/all_to_all | solution.py:181
  34.2 0.3 fusion
  34.5 0.6 broadcast_in_dim.2
  35.1 4.1 %all-to-all-start.2 = ((bf16[32,1,128]{2,1,0:T(2,128)(2,1)}), bf16[32,1,128]{2,1,0:T(2,128)(2,1)S(1)}, u32[]{:S(2)}, u32[]{:S(2)}) async-start(bf16[32,1,128]{2,1,0:T(2,128)(2,1)} %broadcast_in_dim.2), calls=%async_computation.2 | async-start | bytes 32768 | tf_op jit(solution)/shard_map/all_to_all | solution.py:192
  39.2 2.5 %place_rows.1 = bf16[512,1024]{1,0:T(8,128)(2,1)} custom-call(s32[1,256]{1,0:T(1,128)} %get-tuple-element.7.slot, bf16[256,1024]{1,0:T(8,128)(2,1)} %emb.1), custom_call_target="tpu_custom_call" | custom-call | flops 268435456 | bytes 2097152 | tf_op jit(solution)/shard_map/place_rows/pallas_call | solution.py:182
  41.7 2.2 %reshape.42 = bf16[256,2,1024]{2,1,0:T(2,128)(2,1)} reshape(bf16[512,1024]{1,0:T(8,128)(2,1)} %place_rows.1) | data formatting | bytes 2097152 | tf_op jit(solution)/shard_map/reshape | solution.py:190
  43.9 2.4 %all-to-all-done.2 = bf16[32,1,128]{2,1,0:T(2,128)(2,1)S(1)} async-done(((bf16[32,1,128]{2,1,0:T(2,128)(2,1)}), bf16[32,1,128]{2,1,0:T(2,128)(2,1)S(1)}, u32[]{:S(2)}, u32[]{:S(2)}) %all-to-all-start.2) | async-done | bytes 8224 | tf_op jit(solution)/shard_map/all_to_all | solution.py:192
  46.3 6.3 %all-to-all-start = ((bf16[256,2,1024]{2,1,0:T(2,128)(2,1)}), bf16[256,2,1024]{2,1,0:T(2,128)(2,1)S(1)}, u32[]{:S(2)}, u32[]{:S(2)}) async-start(bf16[256,2,1024]{2,1,0:T(2,128)(2,1)} %reshape.42), calls=%async_computation | async-start | bytes 2097152 | tf_op jit(solution)/shard_map/all_to_all | solution.py:190
  52.6 0.6 copy.30
  53.2 0.6 copy.31
  53.8 30.9 %all-to-all-done = bf16[256,2,1024]{2,1,0:T(2,128)(2,1)S(1)} async-done(((bf16[256,2,1024]{2,1,0:T(2,128)(2,1)}), bf16[256,2,1024]{2,1,0:T(2,128)(2,1)S(1)}, u32[]{:S(2)}, u32[]{:S(2)}) %all-to-all-start) | async-done | bytes 1048608 | tf_op jit(solution)/shard_map/all_to_all | solution.py:190
  84.7 0.3 copy.29
  85.0 1.1 %copy.20 = bf16[8,32,2,1024]{3,2,1,0:T(2,128)(2,1)S(1)} copy(bf16[8,32,2,1024]{3,0,1,2:T(8,128)(2,1)S(1)} %bitcast.17) | data formatting | bytes 2097152 | tf_op jit(solution)/shard_map/transpose | solution.py:193
  86.1 1.2 %reshape.44.refs_2_ = bf16[512,1024]{1,0:T(8,128)(2,1)} reshape(bf16[8,32,2,1024]{3,2,1,0:T(2,128)(2,1)S(1)} %copy.20) | data formatting | bytes 2097152 | tf_op jit(solution)/shard_map/reshape | solution.py:193
  87.3 2.9 %select.1 = (f32[1,512]{1,0:T(1,128)}, f32[4,512]{1,0:T(4,128)}) custom-call(s32[4]{0:T(128)} %refs_0_.1, s32[1]{0:T(128)} %bitcast.5.refs_1_, bf16[512,1024]{1,0:T(8,128)(2,1)} %reshape.44.refs_2_, bf16[32,128]{1,0:T(8,128)(2,1)} %bitcast.20, bf16[256,128]{1,0:T(8,128)(2,1)} %bitcast.19), custom_call_target="tpu_custom_call" | custom-call | tf_op jit(solution)/shard_map/select/pallas_call | solution.py:194
Async XLA Ops:
  1.3 0.7 copy-start
  35.1 11.2 %all-to-all-start.2 = ((bf16[32,1,128]{2,1,0:T(2,128)(2,1)}), bf16[32,1,128]{2,1,0:T(2,128)(2,1)S(1)}, u32[]{:S(2)}, u32[]{:S(2)}) async-start(bf16[32,1,128]{2,1,0:T(2,128)(2,1)} %broadcast_in_dim.2), calls=%async_computation.2 | async-start | bytes 32768 | tf_op jit(solution)/shard_map/all_to_all | solution.py:192
  46.3 38.5 %all-to-all-start = ((bf16[256,2,1024]{2,1,0:T(2,128)(2,1)}), bf16[256,2,1024]{2,1,0:T(2,128)(2,1)S(1)}, u32[]{:S(2)}, u32[]{:S(2)}) async-start(bf16[256,2,1024]{2,1,0:T(2,128)(2,1)} %reshape.42), calls=%async_computation | async-start | bytes 2097152 | tf_op jit(solution)/shard_map/all_to_all | solution.py:190

commit v2 on v1

v2 whole, which is shorter than its diff:
```python
import jax
import jax.numpy as jnp
from jax import lax
from jax.experimental import pallas as pl
from jax.experimental.pallas import tpu as pltpu
from jax.sharding import Mesh
from jax.sharding import PartitionSpec as P

ALL = ("z", "x", "y", "core")
PLANE = ("x", "y", "core")
RING = ("x", "y", "core", "z")
RIDGE = 0.1
LANES = 128
F32 = jnp.float32
BF16 = jnp.bfloat16
VMEM = pl.BlockSpec(memory_space=pltpu.VMEM)
SMEM = pl.BlockSpec(memory_space=pltpu.SMEM)


def iota(shape, dim):
    return lax.broadcasted_iota(jnp.int32, shape, dim)


def prep(shards, plane, base, winners, counts, weight, emb, dest, quality, domain, slot_out, quality_out, win_out, picks):
    slots, width = emb.shape
    steps = winners.shape[0]
    square = (slots, slots)
    row, col = iota(square, 0), iota(square, 1)
    dest_row = dest[...].astype(F32)
    across = jnp.broadcast_to(dest_row, square)
    down = jnp.sum(jnp.where(row == col, across, 0.0), axis=1, keepdims=True)
    earlier = (down == across) & (row < col)
    rank = jnp.sum(jnp.where(earlier, 1.0, 0.0), axis=0, keepdims=True)
    lane = iota((1, slots), 1)
    valid = lane < counts[0]
    ring = shards // plane
    to = dest[...]
    to = lax.rem(to, plane) * ring + lax.div(to, plane)
    slot_out[...] = jnp.where(valid, 2 * to + rank.astype(jnp.int32), -1)
    scale = jnp.zeros((1, slots), F32)
    for k in range(weight.shape[0]):
        scale = jnp.where(domain[...] == k, weight[k], scale)
    row_quality = (quality[...] * scale).astype(BF16).astype(F32)
    quality_out[...] = row_quality

    turn = iota((8, slots), 0)
    wanted = jnp.full((8, slots), -1, jnp.int32)
    for t in range(steps):
        wanted = jnp.where(turn == t, winners[t] - base[0], wanted)
    chosen = (iota((8, slots), 1) == wanted) & valid
    spread = jnp.zeros((8, LANES), F32)
    turn_out, lane_out = iota((8, LANES), 0), iota((8, LANES), 1)
    for k, value in enumerate((row_quality, dest_row, rank)):
        mine = jnp.sum(jnp.where(chosen, value, 0.0), axis=1, keepdims=True)
        here = (lane_out == turn_out + k * steps) & (turn_out < steps)
        spread = spread + jnp.where(here, mine, 0.0)
    parts = width // LANES
    picks[...] = jnp.zeros_like(picks)
    picks[steps * parts : steps * parts + 1, :] = jnp.sum(spread, axis=0, keepdims=True)
    picked = jnp.dot(chosen.astype(F32).astype(BF16), emb[...], preferred_element_type=F32)
    for t in range(steps):
        for j in range(parts):
            picks[t * parts + j : t * parts + j + 1, :] = picked[t : t + 1, j * LANES : (j + 1) * LANES]
    win_out[...] = picks[...].astype(BF16)


def place_rows(slot, quality, emb, out):
    rows = out.shape[0]
    slots, width = emb.shape
    block = 128
    for at in range(0, rows, block):
        hit = (iota((block, slots), 0) + at) == slot[...]
        mine = jnp.sum(jnp.where(hit, quality[...], 0.0), axis=1, keepdims=True)
        hot = jnp.where(hit, 1.0, 0.0).astype(BF16)
        out[at : at + block, :width] = jnp.dot(hot, emb[...], preferred_element_type=F32).astype(BF16)
        out[at : at + block, width:] = jnp.broadcast_to(mine, (block, out.shape[1] - width)).astype(BF16)


def select(winners, base, rows, side, relaid, gain_out, chol_out, wide):
    balanced, width = relaid.shape
    steps = chol_out.shape[0]
    parts = width // LANES
    wide[...] = jnp.zeros_like(wide)
    received = side[...].astype(F32)
    for t in range(steps):
        for j in range(parts):
            wide[t : t + 1, j * LANES : (j + 1) * LANES] = received[t * parts + j : t * parts + j + 1, :]
    win = wide[...].astype(BF16)
    nt = (((1,), (1,)), ((), ()))
    relaid[...] = rows[:, :width]
    dots = lax.dot_general(win, rows[:, :width], nt, preferred_element_type=F32)
    gram = lax.dot_general(win, win, nt, preferred_element_type=F32)
    partial = jnp.zeros((balanced, LANES), F32)
    for j in range(parts):
        x = rows[:, j * LANES : (j + 1) * LANES].astype(F32)
        partial = partial + x * x
    ones = jnp.ones((8, LANES), BF16)
    norms = jnp.zeros((8, balanced), F32)
    rest = partial
    for _ in range(3):
        part = rest.astype(BF16)
        rest = rest - part.astype(F32)
        norms = norms + lax.dot_general(ones, part, nt, preferred_element_type=F32)
    norms = norms[0:1, :]
    first = jnp.where(iota((8, LANES), 1) == 0, 1.0, 0.0).astype(BF16)
    quality = lax.dot_general(first, rows[:, width:], nt, preferred_element_type=F32)[0:1, :]

    scalars = received[steps * parts : steps * parts + 1, :]
    win_quality = [scalars[:, t : 1 + t] for t in range(steps)]
    win_dest = [scalars[:, steps + t : 1 + steps + t].astype(jnp.int32) for t in range(steps)]
    win_rank = [scalars[:, 2 * steps + t : 1 + 2 * steps + t].astype(jnp.int32) for t in range(steps)]

    gain = jnp.where(quality > 0, quality * quality * norms / width + RIDGE, 0.0)
    local = iota((1, balanced), 1) + 2 * base[0]
    columns, roots, chol = [], [], []
    for t in range(steps):
        column = []
        for k in range(t):
            cross = win_quality[k] * win_quality[t] * gram[k : k + 1, t : t + 1] / width
            for e in range(k):
                cross = cross - columns[k][e] * column[e]
            column.append(cross / roots[k])
        own_gain = win_quality[t] * win_quality[t] * gram[t : t + 1, t : t + 1] / width + RIDGE
        for k in range(t):
            own_gain = own_gain - column[k] * column[k]
        root = jnp.sqrt(own_gain)
        inner = jnp.zeros((1, balanced), F32)
        for k in range(t):
            inner = inner + chol[k] * column[k]
        place = win_dest[t] * balanced + winners[t] // (balanced // 2) * 2 + win_rank[t]
        hit = jnp.where(local == place, RIDGE, 0.0)
        entry = (quality * win_quality[t] * dots[t : t + 1, :] / width + hit - inner) / root
        gain = gain - entry * entry
        columns.append(column)
        roots.append(root)
        chol.append(entry)
        chol_out[t : t + 1, :] = entry
    gain_out[...] = gain


def gathered(x, axis, rounds):
    size = lax.axis_size(axis)
    for shifts in rounds:
        came = [lax.ppermute(x, axis, [(i, (i + k) % size) for i in range(size)]) for k in shifts]
        for y in came:
            x = x + y
    return x


def body(embeds, quality, domain_ids, domain_weight, dest, counts, winners):
    shards = lax.axis_size(ALL)
    plane = lax.axis_size(PLANE)
    ring = shards // plane
    slots, width = embeds.shape
    steps = winners.shape[0]
    balanced = 2 * slots
    base = (lax.axis_index(ALL) * slots).reshape(1)
    parts = width // LANES
    held = steps * parts + 16
    small = pltpu.CompilerParams(vmem_limit_bytes=12 << 20)

    slot, row_quality, win = pl.pallas_call(
        lambda *refs: prep(shards, plane, *refs),
        in_specs=[SMEM, SMEM, SMEM, SMEM, VMEM, VMEM, VMEM, VMEM],
        out_specs=[VMEM, VMEM, VMEM],
        out_shape=[
            jax.ShapeDtypeStruct((1, slots), jnp.int32),
            jax.ShapeDtypeStruct((1, slots), F32),
            jax.ShapeDtypeStruct((held, LANES), BF16),
        ],
        scratch_shapes=[pltpu.VMEM((held, LANES), F32)],
        compiler_params=small,
        name="prep",
    )(
        base,
        winners,
        counts,
        domain_weight,
        embeds,
        dest.reshape(1, slots),
        quality.reshape(1, slots),
        domain_ids.reshape(1, slots),
    )
    win = gathered(win, "z", ((2, 4, 6), (1,)))
    send = pl.pallas_call(
        place_rows,
        in_specs=[VMEM, VMEM, VMEM],
        out_specs=VMEM,
        out_shape=jax.ShapeDtypeStruct((balanced, width + LANES), BF16),
        compiler_params=small,
        name="place_rows",
        cost_estimate=pl.CostEstimate(flops=2 * balanced * slots * width, bytes_accessed=1 << 21, transcendentals=0),
    )(slot, row_quality, embeds)
    send = send.reshape(shards, 2, width + LANES)
    rows_in = lax.all_to_all(send, RING, 0, 0, tiled=True)
    win = gathered(win, "y", ((1, 2, 3),))
    win = gathered(win, "x", ((1, 2, 3),))
    win = gathered(win, "core", ((1,),))
    rows = rows_in.reshape(plane, ring, 2, width + LANES).swapaxes(0, 1).reshape(balanced, width + LANES)
    relaid, gain, chol = pl.pallas_call(
        select,
        in_specs=[SMEM, SMEM, VMEM, VMEM],
        out_specs=[VMEM, VMEM, VMEM],
        out_shape=[
            jax.ShapeDtypeStruct((balanced, width), BF16),
            jax.ShapeDtypeStruct((1, balanced), F32),
            jax.ShapeDtypeStruct((steps, balanced), F32),
        ],
        scratch_shapes=[pltpu.VMEM((8, width), F32)],
        compiler_params=small,
        name="select",
    )(winners, base, rows, win)
    return relaid, gain.reshape(balanced), chol


def solution(mesh):
    finer = Mesh(mesh.devices.reshape(8, 4, 4, mesh.shape["grp"]), ALL)
    placed = (P(ALL, None), P(ALL), P(ALL), P(), P(ALL), P(ALL), P())
    return jax.shard_map(
        body,
        mesh=finer,
        in_specs=placed,
        out_specs=(P(ALL, None), P(ALL), P(None, ALL)),
        check_vma=False,
    )
```

time: 90.5 us -> 84.8 us (0.937)
  blocking collectives: 28.5 us -> 0 us
  starting transfers between devices: 10.4 us -> 38.3 us
  Pallas kernels: 7.43 us -> 3.62 us
    all_to_all x2 -> x1, waiting for transfers between devices: 33.3 us -> 0.01 us  [body(): rows_in = lax.all_to_all(send, RING, 0, 0, tiled=True)]
    ppermute x0 -> x11, waiting for transfers between devices: none -> 32.4 us  [gathered(): lax.ppermute(x, axis, [(i, (i + k) % size) for i in range(size)])]
    all_to_all x1 -> x0, blocking collectives: 28.5 us -> none  [body(): lax.all_to_all(aux.reshape(shards, 2, LANES), RING, 0, 0, tiled=True)]
    ppermute x0 -> x11, starting transfers between devices: none -> 22.7 us  [gathered(): lax.ppermute(x, axis, [(i, (i + k) % size) for i in range(size)])]
    all_to_all x2 -> x1, starting transfers between devices: 10.4 us -> 15.6 us  [body(): rows_in = lax.all_to_all(send, RING, 0, 0, tiled=True)]
    unnamed x4 -> x16, local copies, waits for them, and re-layouts: 1.88 us -> 5.58 us
    pallas_call x2, Pallas kernels: 5.36 us -> 2.87 us  [the longest x1 2.41 us: body(): pl.pallas_call(select, in_specs=[SMEM, SMEM, VMEM, VMEM], out_specs=[VMEM...]
    reshape x3 -> x2, local copies, waits for them, and re-layouts: 3.58 us -> 1.8 us  [the longest x1 1.31 us: body(): send = send.reshape(shards, 2, width + LANES)]
  transfers between devices with their start and end apart: 2 -> 12, of which waited for: 2 -> 8; matrix products, arithmetic and copies ran while one was open for 4% -> 0% of each run, Pallas kernels for 3% -> 0%
where the time goes in v2:
time: 84.8 us; the launch traced here: 84.4 us
  starting transfers between devices  38.3 us (45%)
  waiting for transfers between devices  32.4 us (38%)
  local copies, waits for them, and re-layouts  8.72 us (10%)
  Pallas kernels  3.62 us (4%)
  between operations  1.38 us (2%)
    ppermute x11, waiting for transfers between devices, gathered(): lax.ppermute(x, axis, [(i, (i + k) % size) for i in range(size)])  32.4 us
    ppermute x11, starting transfers between devices, gathered(): lax.ppermute(x, axis, [(i, (i + k) % size) for i in range(size)])  22.7 us
    all_to_all x1, starting transfers between devices, body(): rows_in = lax.all_to_all(send, RING, 0, 0, tiled=True)  15.6 us
    unnamed x16, local copies, waits for them, and re-layouts  5.58 us
    pallas_call x1, Pallas kernels, body(): pl.pallas_call(select, in_specs=[SMEM, SMEM, VMEM, VMEM], out_specs=[VMEM...  2.41 us
  transfers between devices with their start and end apart: 12, of which 8 were waited for; matrix products, arithmetic and copies ran while one was open for 0% of the time, Pallas kernels for 0%

profile of v2, /device:TPU:1, one launch (start us, length us, event | category | flops | bytes accessed | tf_op | source)
XLA Modules:
  0.0 84.4 jit_solution(17637469068937851443)
XLA Ops:
  1.3 1.0 %copy-done = bf16[256,1024]{1,0:T(8,128)(2,1)S(1)} copy-done((bf16[256,1024]{1,0:T(8,128)(2,1)S(1)}, bf16[256,1024]{1,0:T(8,128)(2,1)}, u32[]{:S(2)}) %copy-start) | copy-done | bytes 524312
  2.3 0.7 copy-done.2
  3.0 0.7 copy-done.4
  3.7 0.7 copy-done.5
  4.3 0.7 copy-done.6
  5.0 0.7 copy-done.7
  5.7 0.8 prep.1
  6.4 1.0 %copy-done.1 = bf16[256,1024]{1,0:T(8,128)(2,1)S(1)} copy-done((bf16[256,1024]{1,0:T(8,128)(2,1)S(1)}, bf16[256,1024]{1,0:T(8,128)(2,1)}, u32[]{:S(2)}) %copy-start.1) | copy-done | bytes 524312
  7.5 0.5 place_rows.1
  8.0 1.3 %reshape.34 = bf16[256,2,1152]{2,1,0:T(2,128)(2,1)} reshape(bf16[512,1152]{1,0:T(8,128)(2,1)S(1)} %place_rows.1) | data formatting | bytes 2359296 | tf_op jit(solution)/shard_map/reshape | solution.py:194
  9.3 15.6 %all-to-all-start = ((bf16[256,2,1152]{2,1,0:T(2,128)(2,1)}), bf16[256,2,1152]{2,1,0:T(2,128)(2,1)S(1)}, u32[]{:S(2)}, u32[]{:S(2)}) async-start(bf16[256,2,1152]{2,1,0:T(2,128)(2,1)} %reshape.34), calls=%async_computation | async-start | bytes 2359296 | tf_op jit(solution)/shard_map/all_to_all | solution.py:195
  24.9 5.0 %collective-permute-start.2 = (bf16[48,128]{1,0:T(8,128)(2,1)S(1)}, bf16[48,128]{1,0:T(8,128)(2,1)S(1)}, u32[]{:S(2)}, u32[]{:S(2)}) collective-permute-start(bf16[48,128]{1,0:T(8,128)(2,1)S(1)} %get-tuple-element.11), channel_id=1, source_target_pairs={{0,192},{32,224},{64,0},{96,32},{128,64},{160,96},{192,128},{224,1... | collective-permute-start | bytes 36872 | tf_op jit(solution)/shard_map/ppermute | solution.py:144
  29.9 1.4 %collective-permute-start.1 = (bf16[48,128]{1,0:T(8,128)(2,1)S(1)}, bf16[48,128]{1,0:T(8,128)(2,1)S(1)}, u32[]{:S(2)}, u32[]{:S(2)}) collective-permute-start(bf16[48,128]{1,0:T(8,128)(2,1)S(1)} %get-tuple-element.11), channel_id=1, source_target_pairs={{0,128},{32,160},{64,192},{96,224},{128,0},{160,32},{192,64},{224,... | collective-permute-start | bytes 36872 | tf_op jit(solution)/shard_map/ppermute | solution.py:144
  31.3 2.3 %collective-permute-start = (bf16[48,128]{1,0:T(8,128)(2,1)S(1)}, bf16[48,128]{1,0:T(8,128)(2,1)S(1)}, u32[]{:S(2)}, u32[]{:S(2)}) collective-permute-start(bf16[48,128]{1,0:T(8,128)(2,1)S(1)} %get-tuple-element.11), channel_id=1, source_target_pairs={{0,64},{32,96},{64,128},{96,160},{128,192},{160,224},{192,0},{224,... | collective-permute-start | bytes 36872 | tf_op jit(solution)/shard_map/ppermute | solution.py:144
  33.6 17.0 %collective-permute-done.2 = bf16[48,128]{1,0:T(8,128)(2,1)S(1)} collective-permute-done((bf16[48,128]{1,0:T(8,128)(2,1)S(1)}, bf16[48,128]{1,0:T(8,128)(2,1)S(1)}, u32[]{:S(2)}, u32[]{:S(2)}) %collective-permute-start.2) | collective-permute-done | bytes 12320 | tf_op jit(solution)/shard_map/ppermute | solution.py:144
  50.6 5.1 %collective-permute-done.1 = bf16[48,128]{1,0:T(8,128)(2,1)S(1)} collective-permute-done((bf16[48,128]{1,0:T(8,128)(2,1)S(1)}, bf16[48,128]{1,0:T(8,128)(2,1)S(1)}, u32[]{:S(2)}, u32[]{:S(2)}) %collective-permute-start.1) | collective-permute-done | bytes 12320 | tf_op jit(solution)/shard_map/ppermute | solution.py:144
  55.7 1.3 %collective-permute-start.3 = (bf16[48,128]{1,0:T(8,128)(2,1)S(1)}, bf16[48,128]{1,0:T(8,128)(2,1)S(1)}, u32[]{:S(2)}, u32[]{:S(2)}) collective-permute-start(bf16[48,128]{1,0:T(8,128)(2,1)S(1)} %add_add_fusion.2), channel_id=1, source_target_pairs={{0,32},{32,64},{64,96},{96,128},{128,160},{160,192},{192,224},{224... | collective-permute-start | bytes 36872 | tf_op jit(solution)/shard_map/ppermute | solution.py:144
  57.0 2.8 %collective-permute-done.3 = bf16[48,128]{1,0:T(8,128)(2,1)S(1)} collective-permute-done((bf16[48,128]{1,0:T(8,128)(2,1)S(1)}, bf16[48,128]{1,0:T(8,128)(2,1)S(1)}, u32[]{:S(2)}, u32[]{:S(2)}) %collective-permute-start.3) | collective-permute-done | bytes 12320 | tf_op jit(solution)/shard_map/ppermute | solution.py:144
  59.9 2.4 %collective-permute-start.6 = (bf16[48,128]{1,0:T(8,128)(2,1)S(1)}, bf16[48,128]{1,0:T(8,128)(2,1)S(1)}, u32[]{:S(2)}, u32[]{:S(2)}) collective-permute-start(bf16[48,128]{1,0:T(8,128)(2,1)S(1)} %add.48), channel_id=1, source_target_pairs={{0,6},{2,0},{4,2},{6,4},{1,7},{3,1},{5,3},{7,5},{8,14},{10,8},{12,... | collective-permute-start | bytes 36872 | tf_op jit(solution)/shard_map/ppermute | solution.py:144
  62.3 0.6 collective-permute-start.5
  62.9 0.5 collective-permute-start.4
  63.4 2.9 %collective-permute-done.5 = bf16[48,128]{1,0:T(8,128)(2,1)S(1)} collective-permute-done((bf16[48,128]{1,0:T(8,128)(2,1)S(1)}, bf16[48,128]{1,0:T(8,128)(2,1)S(1)}, u32[]{:S(2)}, u32[]{:S(2)}) %collective-permute-start.5) | collective-permute-done | bytes 12320 | tf_op jit(solution)/shard_map/ppermute | solution.py:144
  66.7 2.3 %collective-permute-start.9 = (bf16[48,128]{1,0:T(8,128)(2,1)S(1)}, bf16[48,128]{1,0:T(8,128)(2,1)S(1)}, u32[]{:S(2)}, u32[]{:S(2)}) collective-permute-start(bf16[48,128]{1,0:T(8,128)(2,1)S(1)} %add_add_fusion.1), channel_id=1, source_target_pairs={{0,24},{8,0},{16,8},{24,16},{1,25},{9,1},{17,9},{25,17},{2,26},{10... | collective-permute-start | bytes 36872 | tf_op jit(solution)/shard_map/ppermute | solution.py:144
  68.9 0.7 collective-permute-start.8
  69.6 0.5 collective-permute-start.7
  70.1 2.9 %collective-permute-done.8 = bf16[48,128]{1,0:T(8,128)(2,1)S(1)} collective-permute-done((bf16[48,128]{1,0:T(8,128)(2,1)S(1)}, bf16[48,128]{1,0:T(8,128)(2,1)S(1)}, u32[]{:S(2)}, u32[]{:S(2)}) %collective-permute-start.8) | collective-permute-done | bytes 12320 | tf_op jit(solution)/shard_map/ppermute | solution.py:144
  73.0 0.4 collective-permute-done.7
  73.4 5.8 %collective-permute-start.10 = (bf16[48,128]{1,0:T(8,128)(2,1)S(1)}, bf16[48,128]{1,0:T(8,128)(2,1)S(1)}, u32[]{:S(2)}, u32[]{:S(2)}) collective-permute-start(bf16[48,128]{1,0:T(8,128)(2,1)S(1)} %add_add_fusion), channel_id=1, source_target_pairs={{0,1},{1,0},{2,3},{3,2},{4,5},{5,4},{6,7},{7,6},{8,9},{9,8},{10,11... | collective-permute-start | bytes 36872 | tf_op jit(solution)/shard_map/ppermute | solution.py:144
  79.2 0.8 collective-permute-done.10
  80.2 1.2 %copy.13 = bf16[8,32,2,1152]{3,2,1,0:T(2,128)(2,1)S(1)} copy(bf16[8,32,2,1152]{3,0,1,2:T(8,128)(2,1)S(1)} %bitcast.13) | data formatting | bytes 2359296 | tf_op jit(solution)/shard_map/transpose | solution.py:199
  81.4 0.5 reshape.36.rows
  82.0 2.4 %select.1 = (bf16[512,1024]{1,0:T(8,128)(2,1)}, f32[1,512]{1,0:T(1,128)}, f32[4,512]{1,0:T(4,128)}) custom-call(s32[4]{0:T(128)S(1)} %copy-done.3, s32[1]{0:T(128)} %bitcast.refs_0_.base, bf16[512,1152]{1,0:T(8,128)(2,1)S(1)} %reshape.36.rows, bf16[48,128]{1,0:T(8,128)(2,1)S(1)} %add.55.side), custom_call_target="tpu_custom_call" | custom-call | tf_op jit(solution)/shard_map/select/pallas_call | solution.py:200
  (20 shorter events, 0.7 us)
Async XLA Ops:
  1.3 1.0 %copy-start = (bf16[256,1024]{1,0:T(8,128)(2,1)S(1)}, bf16[256,1024]{1,0:T(8,128)(2,1)}, u32[]{:S(2)}) copy-start(bf16[256,1024]{1,0:T(8,128)(2,1)} %emb.1) | copy-start | bytes 1572868
  2.3 0.7 copy-start.2
  3.0 0.7 copy-start.4
  3.7 0.7 copy-start.5
  4.3 0.7 copy-start.6
  5.0 0.7 copy-start.7
  6.4 1.0 %copy-start.1 = (bf16[256,1024]{1,0:T(8,128)(2,1)S(1)}, bf16[256,1024]{1,0:T(8,128)(2,1)}, u32[]{:S(2)}) copy-start(bf16[256,1024]{1,0:T(8,128)(2,1)} %emb.1) | copy-start | bytes 1572868
  9.3 70.7 %all-to-all-start = ((bf16[256,2,1152]{2,1,0:T(2,128)(2,1)}), bf16[256,2,1152]{2,1,0:T(2,128)(2,1)S(1)}, u32[]{:S(2)}, u32[]{:S(2)}) async-start(bf16[256,2,1152]{2,1,0:T(2,128)(2,1)} %reshape.34), calls=%async_computation | async-start | bytes 2359296 | tf_op jit(solution)/shard_map/all_to_all | solution.py:195
  24.9 25.7 %collective-permute-start.2 = (bf16[48,128]{1,0:T(8,128)(2,1)S(1)}, bf16[48,128]{1,0:T(8,128)(2,1)S(1)}, u32[]{:S(2)}, u32[]{:S(2)}) collective-permute-start(bf16[48,128]{1,0:T(8,128)(2,1)S(1)} %get-tuple-element.11), channel_id=1, source_target_pairs={{0,192},{32,224},{64,0},{96,32},{128,64},{160,96},{192,128},{224,1... | collective-permute-start | bytes 36872 | tf_op jit(solution)/shard_map/ppermute | solution.py:144
  29.9 25.8 %collective-permute-start.1 = (bf16[48,128]{1,0:T(8,128)(2,1)S(1)}, bf16[48,128]{1,0:T(8,128)(2,1)S(1)}, u32[]{:S(2)}, u32[]{:S(2)}) collective-permute-start(bf16[48,128]{1,0:T(8,128)(2,1)S(1)} %get-tuple-element.11), channel_id=1, source_target_pairs={{0,128},{32,160},{64,192},{96,224},{128,0},{160,32},{192,64},{224,... | collective-permute-start | bytes 36872 | tf_op jit(solution)/shard_map/ppermute | solution.py:144
  31.3 24.4 %collective-permute-start = (bf16[48,128]{1,0:T(8,128)(2,1)S(1)}, bf16[48,128]{1,0:T(8,128)(2,1)S(1)}, u32[]{:S(2)}, u32[]{:S(2)}) collective-permute-start(bf16[48,128]{1,0:T(8,128)(2,1)S(1)} %get-tuple-element.11), channel_id=1, source_target_pairs={{0,64},{32,96},{64,128},{96,160},{128,192},{160,224},{192,0},{224,... | collective-permute-start | bytes 36872 | tf_op jit(solution)/shard_map/ppermute | solution.py:144
  55.7 4.1 %collective-permute-start.3 = (bf16[48,128]{1,0:T(8,128)(2,1)S(1)}, bf16[48,128]{1,0:T(8,128)(2,1)S(1)}, u32[]{:S(2)}, u32[]{:S(2)}) collective-permute-start(bf16[48,128]{1,0:T(8,128)(2,1)S(1)} %add_add_fusion.2), channel_id=1, source_target_pairs={{0,32},{32,64},{64,96},{96,128},{128,160},{160,192},{192,224},{224... | collective-permute-start | bytes 36872 | tf_op jit(solution)/shard_map/ppermute | solution.py:144
  59.9 3.5 %collective-permute-start.6 = (bf16[48,128]{1,0:T(8,128)(2,1)S(1)}, bf16[48,128]{1,0:T(8,128)(2,1)S(1)}, u32[]{:S(2)}, u32[]{:S(2)}) collective-permute-start(bf16[48,128]{1,0:T(8,128)(2,1)S(1)} %add.48), channel_id=1, source_target_pairs={{0,6},{2,0},{4,2},{6,4},{1,7},{3,1},{5,3},{7,5},{8,14},{10,8},{12,... | collective-permute-start | bytes 36872 | tf_op jit(solution)/shard_map/ppermute | solution.py:144
  62.3 4.0 %collective-permute-start.5 = (bf16[48,128]{1,0:T(8,128)(2,1)S(1)}, bf16[48,128]{1,0:T(8,128)(2,1)S(1)}, u32[]{:S(2)}, u32[]{:S(2)}) collective-permute-start(bf16[48,128]{1,0:T(8,128)(2,1)S(1)} %add.48), channel_id=1, source_target_pairs={{0,4},{2,6},{4,0},{6,2},{1,5},{3,7},{5,1},{7,3},{8,12},{10,14},{12... | collective-permute-start | bytes 36872 | tf_op jit(solution)/shard_map/ppermute | solution.py:144
  62.9 3.8 %collective-permute-start.4 = (bf16[48,128]{1,0:T(8,128)(2,1)S(1)}, bf16[48,128]{1,0:T(8,128)(2,1)S(1)}, u32[]{:S(2)}, u32[]{:S(2)}) collective-permute-start(bf16[48,128]{1,0:T(8,128)(2,1)S(1)} %add.48), channel_id=1, source_target_pairs={{0,2},{2,4},{4,6},{6,0},{1,3},{3,5},{5,7},{7,1},{8,10},{10,12},{12... | collective-permute-start | bytes 36872 | tf_op jit(solution)/shard_map/ppermute | solution.py:144
  66.7 3.4 %collective-permute-start.9 = (bf16[48,128]{1,0:T(8,128)(2,1)S(1)}, bf16[48,128]{1,0:T(8,128)(2,1)S(1)}, u32[]{:S(2)}, u32[]{:S(2)}) collective-permute-start(bf16[48,128]{1,0:T(8,128)(2,1)S(1)} %add_add_fusion.1), channel_id=1, source_target_pairs={{0,24},{8,0},{16,8},{24,16},{1,25},{9,1},{17,9},{25,17},{2,26},{10... | collective-permute-start | bytes 36872 | tf_op jit(solution)/shard_map/ppermute | solution.py:144
  68.9 4.0 %collective-permute-start.8 = (bf16[48,128]{1,0:T(8,128)(2,1)S(1)}, bf16[48,128]{1,0:T(8,128)(2,1)S(1)}, u32[]{:S(2)}, u32[]{:S(2)}) collective-permute-start(bf16[48,128]{1,0:T(8,128)(2,1)S(1)} %add_add_fusion.1), channel_id=1, source_target_pairs={{0,16},{8,24},{16,0},{24,8},{1,17},{9,25},{17,1},{25,9},{2,18},{10... | collective-permute-start | bytes 36872 | tf_op jit(solution)/shard_map/ppermute | solution.py:144
  69.6 3.8 %collective-permute-start.7 = (bf16[48,128]{1,0:T(8,128)(2,1)S(1)}, bf16[48,128]{1,0:T(8,128)(2,1)S(1)}, u32[]{:S(2)}, u32[]{:S(2)}) collective-permute-start(bf16[48,128]{1,0:T(8,128)(2,1)S(1)} %add_add_fusion.1), channel_id=1, source_target_pairs={{0,8},{8,16},{16,24},{24,0},{1,9},{9,17},{17,25},{25,1},{2,10},{10... | collective-permute-start | bytes 36872 | tf_op jit(solution)/shard_map/ppermute | solution.py:144
  73.4 6.7 %collective-permute-start.10 = (bf16[48,128]{1,0:T(8,128)(2,1)S(1)}, bf16[48,128]{1,0:T(8,128)(2,1)S(1)}, u32[]{:S(2)}, u32[]{:S(2)}) collective-permute-start(bf16[48,128]{1,0:T(8,128)(2,1)S(1)} %add_add_fusion), channel_id=1, source_target_pairs={{0,1},{1,0},{2,3},{3,2},{4,5},{5,4},{6,7},{7,6},{8,9},{9,8},{10,11... | collective-permute-start | bytes 36872 | tf_op jit(solution)/shard_map/ppermute | solution.py:144
  81.4 0.7 copy-start.3

commit v3 on v2

v3 whole, which is shorter than its diff:
```python
import jax
import jax.numpy as jnp
from jax import lax
from jax.experimental import pallas as pl
from jax.experimental.pallas import tpu as pltpu
from jax.sharding import Mesh
from jax.sharding import PartitionSpec as P

ALL = ("z", "x", "y", "core")
PLANE = ("x", "y", "core")
RIDGE = 0.1
LANES = 128
HALF = 64
F32 = jnp.float32
BF16 = jnp.bfloat16
VMEM = pl.BlockSpec(memory_space=pltpu.VMEM)
SMEM = pl.BlockSpec(memory_space=pltpu.SMEM)
HBM = pl.BlockSpec(memory_space=pltpu.HBM)


def iota(shape, dim):
    return lax.broadcasted_iota(jnp.int32, shape, dim)


def prep(base, winners, counts, weight, emb, dest, quality, domain, table_out, piece_out):
    slots, width = emb.shape
    steps = winners.shape[0]
    square = (slots, slots)
    row, col = iota(square, 0), iota(square, 1)
    dest_row = dest[...].astype(F32)
    across = jnp.broadcast_to(dest_row, square)
    down = jnp.sum(jnp.where(row == col, across, 0.0), axis=1, keepdims=True)
    earlier = (down == across) & (row < col)
    rank = jnp.sum(jnp.where(earlier, 1.0, 0.0), axis=0, keepdims=True)
    lane = iota((1, slots), 1)
    valid = lane < counts[0]
    table_out[...] = jnp.zeros_like(table_out)
    table_out[0:1, :] = jnp.where(valid, 2.0 * dest_row + rank, -1.0)
    scale = jnp.zeros((1, slots), F32)
    for k in range(weight.shape[0]):
        scale = jnp.where(domain[...] == k, weight[k], scale)
    row_quality = (quality[...] * scale).astype(BF16).astype(F32)
    table_out[1:2, :] = row_quality

    turn = iota((8, slots), 0)
    wanted = jnp.full((8, slots), -1, jnp.int32)
    for t in range(steps):
        wanted = jnp.where(turn == t, winners[t] - base[0], wanted)
    chosen = (iota((8, slots), 1) == wanted) & valid
    spread = jnp.zeros((8, LANES), F32)
    turn_out, lane_out = iota((8, LANES), 0), iota((8, LANES), 1)
    for k, value in enumerate((row_quality, dest_row, rank)):
        mine = jnp.sum(jnp.where(chosen, value, 0.0), axis=1, keepdims=True)
        here = (lane_out == turn_out + (HALF + 1 + k * steps)) & (turn_out < steps)
        spread = spread + jnp.where(here, mine, 0.0)
    table_out[2:3, :LANES] = jnp.sum(spread, axis=0, keepdims=True)
    parts = width // LANES
    picked = jnp.dot(chosen.astype(F32).astype(BF16), emb[...], preferred_element_type=F32)
    for t in range(steps):
        for j in range(parts):
            at = t * parts + j
            piece_out[at : at + 1, :] = picked[t : t + 1, j * LANES : (j + 1) * LANES]


def place_rows(table_in, pieces, emb_in, out, table, emb, sems):
    copies = (pltpu.make_async_copy(emb_in, emb, sems.at[0]), pltpu.make_async_copy(table_in, table, sems.at[1]))
    for copy in copies:
        copy.start()
    rows = out.shape[0]
    slots, width = emb.shape
    block = 128
    shape = (block, LANES)
    lane = iota(shape, 1)
    even = lax.rem(iota(shape, 0), 2) == 0
    piece = jnp.sum(pieces[...].astype(F32), axis=0, keepdims=True)
    low, high = lane < HALF, lane >= HALF
    for copy in copies:
        copy.wait()
    slot = table[0:1, :].astype(jnp.int32)
    quality = table[1:2, :]
    scalars = table[2:3, :LANES]
    fixed = jnp.where(even, jnp.where(low, piece, scalars), jnp.where(high, piece, 0.0))
    holds = lane == jnp.where(even, HALF, 0)
    for at in range(0, rows, block):
        hit = (iota((block, slots), 0) + at) == slot
        mine = jnp.sum(jnp.where(hit, quality, 0.0), axis=1, keepdims=True)
        hot = jnp.where(hit, 1.0, 0.0).astype(BF16)
        out[at : at + block, :width] = jnp.dot(hot, emb[...], preferred_element_type=F32).astype(BF16)
        out[at : at + block, width:] = jnp.where(holds, mine, fixed).astype(BF16)


def select(plane, winners, base, rows, relaid, gain_out, chol_out, wide):
    balanced, width = relaid.shape
    steps = chol_out.shape[0]
    parts = width // LANES
    nt = (((1,), (1,)), ((), ()))
    side = rows[:, width:]
    lane = iota((8, LANES), 1)
    turn = iota((8, LANES), 0)
    holds = (lane == jnp.where(turn == 0, HALF, 0)) & (turn < 2)
    both = lax.dot_general(jnp.where(holds, 1.0, 0.0).astype(BF16), side, nt, preferred_element_type=F32)
    odd = lax.rem(iota((1, balanced), 1), 2) == 1
    quality = jnp.where(odd, both[1:2, :], both[0:1, :])

    total = jnp.zeros((2 * plane, LANES), F32)
    for k in range(balanced // (2 * plane)):
        total = total + side[2 * plane * k : 2 * plane * (k + 1), :].astype(F32)
    even = lax.rem(iota((2 * plane, LANES), 0), 2) == 0
    scalars = jnp.sum(jnp.where(even, total, 0.0), axis=0, keepdims=True)
    wide[...] = jnp.zeros_like(wide)
    low = iota((1, LANES), 1) < HALF
    for t in range(steps):
        for j in range(parts):
            at = 2 * (t * parts + j)
            wide[t : t + 1, j * LANES : (j + 1) * LANES] = jnp.where(low, total[at : at + 1, :], total[at + 1 : at + 2, :])
    win = wide[...].astype(BF16)
    relaid[...] = rows[:, :width]
    dots = lax.dot_general(win, rows[:, :width], nt, preferred_element_type=F32)
    gram = lax.dot_general(win, win, nt, preferred_element_type=F32)
    partial = jnp.zeros((balanced, LANES), F32)
    for j in range(parts):
        x = rows[:, j * LANES : (j + 1) * LANES].astype(F32)
        partial = partial + x * x
    ones = jnp.ones((8, LANES), BF16)
    norms = jnp.zeros((8, balanced), F32)
    rest = partial
    for _ in range(3):
        part = rest.astype(BF16)
        rest = rest - part.astype(F32)
        norms = norms + lax.dot_general(ones, part, nt, preferred_element_type=F32)
    norms = norms[0:1, :]

    at = HALF + 1
    win_quality = [scalars[:, at + t : at + 1 + t] for t in range(steps)]
    win_dest = [scalars[:, at + steps + t : at + 1 + steps + t].astype(jnp.int32) for t in range(steps)]
    win_rank = [scalars[:, at + 2 * steps + t : at + 1 + 2 * steps + t].astype(jnp.int32) for t in range(steps)]

    gain = jnp.where(quality > 0, quality * quality * norms / width + RIDGE, 0.0)
    local = iota((1, balanced), 1) + 2 * base[0]
    columns, roots, chol = [], [], []
    for t in range(steps):
        column = []
        for k in range(t):
            cross = win_quality[k] * win_quality[t] * gram[k : k + 1, t : t + 1] / width
            for e in range(k):
                cross = cross - columns[k][e] * column[e]
            column.append(cross / roots[k])
        own_gain = win_quality[t] * win_quality[t] * gram[t : t + 1, t : t + 1] / width + RIDGE
        for k in range(t):
            own_gain = own_gain - column[k] * column[k]
        root = jnp.sqrt(own_gain)
        inner = jnp.zeros((1, balanced), F32)
        for k in range(t):
            inner = inner + chol[k] * column[k]
        place = win_dest[t] * balanced + winners[t] // (balanced // 2) * 2 + win_rank[t]
        hit = jnp.where(local == place, RIDGE, 0.0)
        entry = (quality * win_quality[t] * dots[t : t + 1, :] / width + hit - inner) / root
        gain = gain - entry * entry
        columns.append(column)
        roots.append(root)
        chol.append(entry)
        chol_out[t : t + 1, :] = entry
    gain_out[...] = gain


def body(embeds, quality, domain_ids, domain_weight, dest, counts, winners):
    shards = lax.axis_size(ALL)
    plane = lax.axis_size(PLANE)
    slots, width = embeds.shape
    steps = winners.shape[0]
    balanced = 2 * slots
    base = (lax.axis_index(ALL) * slots).reshape(1)
    small = pltpu.CompilerParams(vmem_limit_bytes=12 << 20)

    table, pieces = pl.pallas_call(
        prep,
        in_specs=[SMEM, SMEM, SMEM, SMEM, VMEM, VMEM, VMEM, VMEM],
        out_specs=[VMEM, VMEM],
        out_shape=[
            jax.ShapeDtypeStruct((8, slots), F32),
            jax.ShapeDtypeStruct((plane, LANES), F32),
        ],
        name="prep",
    )(
        base,
        winners,
        counts,
        domain_weight,
        embeds,
        dest.reshape(1, slots),
        quality.reshape(1, slots),
        domain_ids.reshape(1, slots),
    )
    pieces = pieces.astype(BF16).reshape(plane, 1, LANES)
    pieces = lax.all_to_all(pieces, PLANE, 0, 0, tiled=True).reshape(plane, LANES)
    send = pl.pallas_call(
        place_rows,
        in_specs=[HBM, VMEM, HBM],
        out_specs=VMEM,
        out_shape=jax.ShapeDtypeStruct((balanced, width + LANES), BF16),
        scratch_shapes=[
            pltpu.VMEM((8, slots), F32),
            pltpu.VMEM((slots, width), BF16),
            pltpu.SemaphoreType.DMA((2,)),
        ],
        compiler_params=small,
        name="place_rows",
    )(table, pieces, embeds)
    send = send.reshape(shards, 2, width + LANES)
    rows = lax.all_to_all(send, ALL, 0, 0, tiled=True).reshape(balanced, width + LANES)
    relaid, gain, chol = pl.pallas_call(
        lambda *refs: select(plane, *refs),
        in_specs=[SMEM, SMEM, VMEM],
        out_specs=[VMEM, VMEM, VMEM],
        out_shape=[
            jax.ShapeDtypeStruct((balanced, width), BF16),
            jax.ShapeDtypeStruct((1, balanced), F32),
            jax.ShapeDtypeStruct((steps, balanced), F32),
        ],
        scratch_shapes=[pltpu.VMEM((8, width), F32)],
        compiler_params=small,
        name="select",
    )(winners, base, rows)
    return relaid, gain.reshape(balanced), chol


def solution(mesh):
    finer = Mesh(mesh.devices.reshape(8, 4, 4, mesh.shape["grp"]), ALL)
    placed = (P(ALL, None), P(ALL), P(ALL), P(), P(ALL), P(ALL), P())
    return jax.shard_map(
        body,
        mesh=finer,
        in_specs=placed,
        out_specs=(P(ALL, None), P(ALL), P(None, ALL)),
        check_vma=False,
    )
```

time: 84.8 us -> 69.9 us (0.82)
  blocking collectives: 0 us -> 59.8 us
  starting transfers between devices: 38.3 us -> 0 us
  waiting for transfers between devices: 32.4 us -> 0 us
  local copies, waits for them, and re-layouts: 8.72 us -> 2.89 us
  Pallas kernels: 3.62 us -> 4.83 us
    all_to_all x0 -> x2, blocking collectives: none -> 59.8 us  [the longest x1 44.4 us: body(): lax.all_to_all(send, ALL, 0, 0, tiled=True).reshape(balanced, width + LANES)]
    ppermute x11 -> x0, waiting for transfers between devices: 32.4 us -> none  [gathered(): lax.ppermute(x, axis, [(i, (i + k) % size) for i in range(size)])]
    ppermute x11 -> x0, starting transfers between devices: 22.7 us -> none  [gathered(): lax.ppermute(x, axis, [(i, (i + k) % size) for i in range(size)])]
    all_to_all x1 -> x0, starting transfers between devices: 15.6 us -> none  [body(): rows_in = lax.all_to_all(send, RING, 0, 0, tiled=True)]
    unnamed x16 -> x7, local copies, waits for them, and re-layouts: 5.58 us -> 1.92 us
    transpose x1 -> x0, local copies, waits for them, and re-layouts: 1.21 us -> none  [body(): rows_in.reshape(plane, ring, 2, width + LANES).swapaxes(0, 1)]
    pallas_call x3, Pallas kernels: 3.62 us -> 4.83 us  [the longest x1 2.42 us: body(): pl.pallas_call(lambda *refs: select(plane, *refs), in_specs=[SMEM, SMEM,...]
  transfers between devices with their start and end apart: 12 -> 0, of which waited for: 8 -> 0; matrix products, arithmetic and copies ran while one was open for 0% -> 0% of each run, Pallas kernels for 0% -> 0%
where the time goes in v3:
time: 69.9 us; the launch traced here: 69.5 us
  blocking collectives  59.8 us (86%)
  Pallas kernels  4.83 us (7%)
  local copies, waits for them, and re-layouts  2.89 us (4%)
  between operations  1.32 us (2%)
  other arithmetic  0.72 us (1%)
    all_to_all x1, blocking collectives, body(): lax.all_to_all(send, ALL, 0, 0, tiled=True).reshape(balanced, width + LANES)  44.4 us
    all_to_all x1, blocking collectives, body(): lax.all_to_all(pieces, PLANE, 0, 0, tiled=True).reshape(plane, LANES)  15.3 us
    pallas_call x1, Pallas kernels, body(): pl.pallas_call(lambda *refs: select(plane, *refs), in_specs=[SMEM, SMEM,...  2.42 us
    unnamed x7, local copies, waits for them, and re-layouts  1.92 us
    pallas_call x1, Pallas kernels, body(): pl.pallas_call(prep, in_specs=[SMEM, SMEM, SMEM, SMEM, VMEM, VMEM, VMEM,...  1.88 us

profile of v3, /device:TPU:1, one launch (start us, length us, event | category | flops | bytes accessed | tf_op | source)
XLA Modules:
  0.0 69.5 jit_solution(7558544481005005771)
XLA Ops:
  1.3 1.9 %prep.1 = (f32[8,256]{1,0:T(8,128)}, f32[32,128]{1,0:T(8,128)}) custom-call(s32[1]{0:T(128)} %bitcast.base.refs_1_, s32[4]{0:T(128)} %refs_0_.1, s32[1]{0:T(128)S(6)} %copy.15.counts, f32[16]{0:T(128)} %weight.1, bf16[256,1024]{1,0:T(8,128)(2,1)} %emb_in.1, s32[1,256]{1,0:T(1,128)} %bitcast.11, f32[1,256]{1,0:T(1,128)} %bitcast.12, s32[1,256]{1,0:T(1,128)} %bitcast.13), custom_call_target="tpu_custom_call" | custom-call | tf_op jit(solution)/shard_map/prep/pallas_call | solution.py:175
  3.2 0.7 %convert_bitcast_fusion = bf16[32,1,128]{2,0,1:T(8,128)(2,1)S(1)} fusion(f32[32,128]{1,0:T(8,128)} %get-tuple-element.9), kind=kLoop, calls=%fused_computation.1 | loop fusion | flops 4096 | bytes 24576 | tf_op jit(solution)/shard_map/reshape | solution.py:194
  3.9 15.3 %all_to_all.10 = bf16[32,1,128]{2,1,0:T(2,128)(2,1)S(1)} all-to-all(bf16[32,1,128]{2,1,0:T(2,128)(2,1)S(1)} %copy.11), channel_id=1, replica_groups=mesh['z'=8,'x'=4,'y'=4,'core'=2] {'x','y','core'}, dimensions={0} | all-to-all | bytes 16384 | tf_op jit(solution)/shard_map/all_to_all | solution.py:195
  19.3 0.0 copy-start
  19.3 1.0 %copy-done = bf16[256,1024]{1,0:T(8,128)(2,1)S(1)} copy-done((bf16[256,1024]{1,0:T(8,128)(2,1)S(1)}, bf16[256,1024]{1,0:T(8,128)(2,1)}, u32[]{:S(2)}) %copy-start) | copy-done | bytes 524312
  20.3 0.0 copy-start.1
  20.3 0.7 copy-done.1
  21.0 0.5 place_rows.1
  21.5 0.5 reshape.39
  22.0 44.4 %all_to_all.11 = bf16[256,2,1152]{2,1,0:T(2,128)(2,1)S(1)} all-to-all(bf16[256,2,1152]{2,1,0:T(2,128)(2,1)S(1)} %reshape.39), channel_id=1, replica_groups=mesh['z'=8,'x'=4,'y'=4,'core'=2] {'z','x','y','core'}, dimensions={0} | all-to-all | bytes 2359296 | tf_op jit(solution)/shard_map/all_to_all | solution.py:210
  66.5 0.0 copy-start.2
  66.5 0.5 reshape.40.refs_2_
  66.9 0.2 copy-done.2
  67.1 2.4 %select.1 = (bf16[512,1024]{1,0:T(8,128)(2,1)}, f32[1,512]{1,0:T(1,128)}, f32[4,512]{1,0:T(4,128)}) custom-call(s32[4]{0:T(128)S(1)} %copy-done.2, s32[1]{0:T(128)} %bitcast.base.refs_1_, bf16[512,1152]{1,0:T(8,128)(2,1)S(1)} %reshape.40.refs_2_), custom_call_target="tpu_custom_call" | custom-call | tf_op jit(solution)/shard_map/select/pallas_call | solution.py:211
  (2 shorter events, 0.0 us)
Async XLA Ops:
  19.3 1.0 %copy-start = (bf16[256,1024]{1,0:T(8,128)(2,1)S(1)}, bf16[256,1024]{1,0:T(8,128)(2,1)}, u32[]{:S(2)}) copy-start(bf16[256,1024]{1,0:T(8,128)(2,1)} %emb_in.1) | copy-start | bytes 1572868
  20.3 0.7 %copy-start.1 = (f32[8,256]{1,0:T(8,128)S(1)}, f32[8,256]{1,0:T(8,128)}, u32[]{:S(2)}) copy-start(f32[8,256]{1,0:T(8,128)} %get-tuple-element.8.table_in) | copy-start | bytes 24580
  66.5 0.7 copy-start.2

commit v4 on v2

--- a/solution.py
+++ b/solution.py
@@ -7,8 +7,6 @@
 from jax.sharding import PartitionSpec as P
 
 ALL = ("z", "x", "y", "core")
-PLANE = ("x", "y", "core")
-RING = ("x", "y", "core", "z")
 RIDGE = 0.1
 LANES = 128
 F32 = jnp.float32
@@ -21,9 +19,11 @@
     return lax.broadcasted_iota(jnp.int32, shape, dim)
 
 
-def prep(shards, plane, base, winners, counts, weight, emb, dest, quality, domain, slot_out, quality_out, win_out, picks):
+def place(base, winners, counts, weight, emb, dest, quality, domain, out, win_out, picks):
     slots, width = emb.shape
+    rows = out.shape[0]
     steps = winners.shape[0]
+    parts = width // LANES
     square = (slots, slots)
     row, col = iota(square, 0), iota(square, 1)
     dest_row = dest[...].astype(F32)
@@ -33,15 +33,11 @@
     rank = jnp.sum(jnp.where(earlier, 1.0, 0.0), axis=0, keepdims=True)
     lane = iota((1, slots), 1)
     valid = lane < counts[0]
-    ring = shards // plane
-    to = dest[...]
-    to = lax.rem(to, plane) * ring + lax.div(to, plane)
-    slot_out[...] = jnp.where(valid, 2 * to + rank.astype(jnp.int32), -1)
+    slot = jnp.where(valid, 2 * dest[...] + rank.astype(jnp.int32), -1)
     scale = jnp.zeros((1, slots), F32)
     for k in range(weight.shape[0]):
         scale = jnp.where(domain[...] == k, weight[k], scale)
     row_quality = (quality[...] * scale).astype(BF16).astype(F32)
-    quality_out[...] = row_quality
 
     turn = iota((8, slots), 0)
     wanted = jnp.full((8, slots), -1, jnp.int32)
@@ -54,7 +50,6 @@
         mine = jnp.sum(jnp.where(chosen, value, 0.0), axis=1, keepdims=True)
         here = (lane_out == turn_out + k * steps) & (turn_out < steps)
         spread = spread + jnp.where(here, mine, 0.0)
-    parts = width // LANES
     picks[...] = jnp.zeros_like(picks)
     picks[steps * parts : steps * parts + 1, :] = jnp.sum(spread, axis=0, keepdims=True)
     picked = jnp.dot(chosen.astype(F32).astype(BF16), emb[...], preferred_element_type=F32)
@@ -63,14 +58,10 @@
             picks[t * parts + j : t * parts + j + 1, :] = picked[t : t + 1, j * LANES : (j + 1) * LANES]
     win_out[...] = picks[...].astype(BF16)
 
-
-def place_rows(slot, quality, emb, out):
-    rows = out.shape[0]
-    slots, width = emb.shape
     block = 128
     for at in range(0, rows, block):
-        hit = (iota((block, slots), 0) + at) == slot[...]
-        mine = jnp.sum(jnp.where(hit, quality[...], 0.0), axis=1, keepdims=True)
+        hit = (iota((block, slots), 0) + at) == slot
+        mine = jnp.sum(jnp.where(hit, row_quality, 0.0), axis=1, keepdims=True)
         hot = jnp.where(hit, 1.0, 0.0).astype(BF16)
         out[at : at + block, :width] = jnp.dot(hot, emb[...], preferred_element_type=F32).astype(BF16)
         out[at : at + block, width:] = jnp.broadcast_to(mine, (block, out.shape[1] - width)).astype(BF16)
@@ -149,28 +140,23 @@
 
 def body(embeds, quality, domain_ids, domain_weight, dest, counts, winners):
     shards = lax.axis_size(ALL)
-    plane = lax.axis_size(PLANE)
-    ring = shards // plane
     slots, width = embeds.shape
     steps = winners.shape[0]
     balanced = 2 * slots
     base = (lax.axis_index(ALL) * slots).reshape(1)
-    parts = width // LANES
-    held = steps * parts + 16
-    small = pltpu.CompilerParams(vmem_limit_bytes=12 << 20)
-
-    slot, row_quality, win = pl.pallas_call(
-        lambda *refs: prep(shards, plane, *refs),
+    broad = width + LANES
+    held = steps * (width // LANES) + 8
+
+    send, win = pl.pallas_call(
+        place,
         in_specs=[SMEM, SMEM, SMEM, SMEM, VMEM, VMEM, VMEM, VMEM],
-        out_specs=[VMEM, VMEM, VMEM],
+        out_specs=[VMEM, VMEM],
         out_shape=[
-            jax.ShapeDtypeStruct((1, slots), jnp.int32),
-            jax.ShapeDtypeStruct((1, slots), F32),
+            jax.ShapeDtypeStruct((balanced, broad), BF16),
             jax.ShapeDtypeStruct((held, LANES), BF16),
         ],
         scratch_shapes=[pltpu.VMEM((held, LANES), F32)],
-        compiler_params=small,
-        name="prep",
+        name="place",
     )(
         base,
         winners,
@@ -181,22 +167,11 @@
         quality.reshape(1, slots),
         domain_ids.reshape(1, slots),
     )
-    win = gathered(win, "z", ((2, 4, 6), (1,)))
-    send = pl.pallas_call(
-        place_rows,
-        in_specs=[VMEM, VMEM, VMEM],
-        out_specs=VMEM,
-        out_shape=jax.ShapeDtypeStruct((balanced, width + LANES), BF16),
-        compiler_params=small,
-        name="place_rows",
-        cost_estimate=pl.CostEstimate(flops=2 * balanced * slots * width, bytes_accessed=1 << 21, transcendentals=0),
-    )(slot, row_quality, embeds)
-    send = send.reshape(shards, 2, width + LANES)
-    rows_in = lax.all_to_all(send, RING, 0, 0, tiled=True)
+    rows = lax.all_to_all(send.reshape(shards, 2, broad), ALL, 0, 0, tiled=True).reshape(balanced, broad)
+    win = gathered(win, "core", ((1,),))
     win = gathered(win, "y", ((1, 2, 3),))
     win = gathered(win, "x", ((1, 2, 3),))
-    win = gathered(win, "core", ((1,),))
-    rows = rows_in.reshape(plane, ring, 2, width + LANES).swapaxes(0, 1).reshape(balanced, width + LANES)
+    win = gathered(win, "z", ((2, 4, 6), (1,)))
     relaid, gain, chol = pl.pallas_call(
         select,
         in_specs=[SMEM, SMEM, VMEM, VMEM],
@@ -207,7 +182,7 @@
             jax.ShapeDtypeStruct((steps, balanced), F32),
         ],
         scratch_shapes=[pltpu.VMEM((8, width), F32)],
-        compiler_params=small,
+        compiler_params=pltpu.CompilerParams(vmem_limit_bytes=12 << 20),
         name="select",
     )(winners, base, rows, win)
     return relaid, gain.reshape(balanced), chol

time: 84.8 us -> 62 us (0.73)
  waiting for transfers between devices: 32.4 us -> 17.3 us
  starting transfers between devices: 38.3 us -> 33.1 us
  local copies, waits for them, and re-layouts: 8.72 us -> 4.26 us
  Pallas kernels: 3.62 us -> 5.09 us
    ppermute x11, waiting for transfers between devices: 32.4 us -> 17.3 us  [gathered(): lax.ppermute(x, axis, [(i, (i + k) % size) for i in range(size)])]
    unnamed x16 -> x4, local copies, waits for them, and re-layouts: 5.58 us -> 0.15 us
    ppermute x11, starting transfers between devices: 22.7 us -> 17.5 us  [gathered(): lax.ppermute(x, axis, [(i, (i + k) % size) for i in range(size)])]
    reshape x2, local copies, waits for them, and re-layouts: 1.8 us -> 4.11 us  [the longest x1 3.62 us: body(): send.reshape(shards, 2, broad)]
    pallas_call x2 -> x1, Pallas kernels: 1.21 us -> 2.68 us  [body(): pl.pallas_call(place, in_specs=[SMEM, SMEM, SMEM, SMEM, VMEM, VMEM, VMEM,...]
    transpose x1 -> x0, local copies, waits for them, and re-layouts: 1.21 us -> none  [body(): rows_in.reshape(plane, ring, 2, width + LANES).swapaxes(0, 1)]
  transfers between devices with their start and end apart: 12 -> 12, of which waited for: 8 -> 9; matrix products, arithmetic and copies ran while one was open for 0% -> 0% of each run, Pallas kernels for 0% -> 0%
where the time goes in v4:
time: 62 us; the launch traced here: 61.2 us
  starting transfers between devices  33.1 us (53%)
  waiting for transfers between devices  17.3 us (28%)
  Pallas kernels  5.09 us (8%)
  local copies, waits for them, and re-layouts  4.26 us (7%)
  between operations  1.35 us (2%)
    ppermute x11, starting transfers between devices, gathered(): lax.ppermute(x, axis, [(i, (i + k) % size) for i in range(size)])  17.5 us
    ppermute x11, waiting for transfers between devices, gathered(): lax.ppermute(x, axis, [(i, (i + k) % size) for i in range(size)])  17.3 us
    all_to_all x1, starting transfers between devices, body(): lax.all_to_all(send.reshape(shards, 2, broad), ALL, 0, 0, tiled=True)  15.6 us
    reshape x1, local copies, waits for them, and re-layouts, body(): send.reshape(shards, 2, broad)  3.62 us
    pallas_call x1, Pallas kernels, body(): pl.pallas_call(place, in_specs=[SMEM, SMEM, SMEM, SMEM, VMEM, VMEM, VMEM,...  2.68 us
    pallas_call x1, Pallas kernels, body(): pl.pallas_call(select, in_specs=[SMEM, SMEM, VMEM, VMEM], out_specs=[VMEM...  2.41 us
  transfers between devices with their start and end apart: 12, of which 9 were waited for; matrix products, arithmetic and copies ran while one was open for 0% of the time, Pallas kernels for 0%

profile of v4, /device:TPU:1, one launch (start us, length us, event | category | flops | bytes accessed | tf_op | source)
XLA Modules:
  0.0 61.2 jit_solution(5837379681171787630)
XLA Ops:
  1.3 2.7 %place.1 = (bf16[512,1152]{1,0:T(8,128)(2,1)}, bf16[40,128]{1,0:T(8,128)(2,1)}) custom-call(s32[1]{0:T(128)} %bitcast.base, s32[4]{0:T(128)} %winners.3, s32[1]{0:T(128)S(6)} %copy.10.counts, f32[16]{0:T(128)} %weight.1, bf16[256,1024]{1,0:T(8,128)(2,1)} %emb.1, s32[1,256]{1,0:T(1,128)} %bitcast.5, f32[1,256]{1,0:T(1,128)} %bitcast.6, s32[1,256]{1,0:T(1,128)} %bitcast.7), custom_call_target="tpu_custom_call" | custom-call | tf_op jit(solution)/shard_map/place/pallas_call | solution.py:150
  4.0 3.6 %reshape.31 = bf16[256,2,1152]{2,1,0:T(2,128)(2,1)} reshape(bf16[512,1152]{1,0:T(8,128)(2,1)} %get-tuple-element.8) | data formatting | bytes 2359296 | tf_op jit(solution)/shard_map/reshape | solution.py:170
  7.6 0.0 copy-start.1
  7.6 15.6 %all-to-all-start = ((bf16[256,2,1152]{2,1,0:T(2,128)(2,1)}), bf16[256,2,1152]{2,1,0:T(2,128)(2,1)S(1)}, u32[]{:S(2)}, u32[]{:S(2)}) async-start(bf16[256,2,1152]{2,1,0:T(2,128)(2,1)} %reshape.31), calls=%async_computation | async-start | bytes 2359296 | tf_op jit(solution)/shard_map/all_to_all | solution.py:170
  23.3 0.0 copy-done.1
  23.3 2.2 %collective-permute-start = (bf16[40,128]{1,0:T(8,128)(2,1)S(1)}, bf16[40,128]{1,0:T(8,128)(2,1)S(1)}, u32[]{:S(2)}, u32[]{:S(2)}) collective-permute-start(bf16[40,128]{1,0:T(8,128)(2,1)S(1)} %copy-done.1), channel_id=1, source_target_pairs={{0,1},{1,0},{2,3},{3,2},{4,5},{5,4},{6,7},{7,6},{8,9},{9,8},{10,11... | collective-permute-start | bytes 30728 | tf_op jit(solution)/shard_map/ppermute | solution.py:135
  25.5 0.8 %collective-permute-done = bf16[40,128]{1,0:T(8,128)(2,1)S(1)} collective-permute-done((bf16[40,128]{1,0:T(8,128)(2,1)S(1)}, bf16[40,128]{1,0:T(8,128)(2,1)S(1)}, u32[]{:S(2)}, u32[]{:S(2)}) %collective-permute-start) | collective-permute-done | bytes 10272 | tf_op jit(solution)/shard_map/ppermute | solution.py:135
  26.3 0.9 %collective-permute-start.3 = (bf16[40,128]{1,0:T(8,128)(2,1)S(1)}, bf16[40,128]{1,0:T(8,128)(2,1)S(1)}, u32[]{:S(2)}, u32[]{:S(2)}) collective-permute-start(bf16[40,128]{1,0:T(8,128)(2,1)S(1)} %add.45), channel_id=1, source_target_pairs={{0,6},{2,0},{4,2},{6,4},{1,7},{3,1},{5,3},{7,5},{8,14},{10,8},{12,... | collective-permute-start | bytes 30728 | tf_op jit(solution)/shard_map/ppermute | solution.py:135
  27.2 0.5 collective-permute-start.2
  27.8 0.6 collective-permute-start.1
  28.4 0.8 %collective-permute-done.3 = bf16[40,128]{1,0:T(8,128)(2,1)S(1)} collective-permute-done((bf16[40,128]{1,0:T(8,128)(2,1)S(1)}, bf16[40,128]{1,0:T(8,128)(2,1)S(1)}, u32[]{:S(2)}, u32[]{:S(2)}) %collective-permute-start.3) | collective-permute-done | bytes 10272 | tf_op jit(solution)/shard_map/ppermute | solution.py:135
  29.2 2.4 %collective-permute-done.2 = bf16[40,128]{1,0:T(8,128)(2,1)S(1)} collective-permute-done((bf16[40,128]{1,0:T(8,128)(2,1)S(1)}, bf16[40,128]{1,0:T(8,128)(2,1)S(1)}, u32[]{:S(2)}, u32[]{:S(2)}) %collective-permute-start.2) | collective-permute-done | bytes 10272 | tf_op jit(solution)/shard_map/ppermute | solution.py:135
  31.6 0.2 collective-permute-done.1
  31.8 2.6 %collective-permute-start.6 = (bf16[40,128]{1,0:T(8,128)(2,1)S(1)}, bf16[40,128]{1,0:T(8,128)(2,1)S(1)}, u32[]{:S(2)}, u32[]{:S(2)}) collective-permute-start(bf16[40,128]{1,0:T(8,128)(2,1)S(1)} %add_add_fusion.2), channel_id=1, source_target_pairs={{0,24},{8,0},{16,8},{24,16},{1,25},{9,1},{17,9},{25,17},{2,26},{10... | collective-permute-start | bytes 30728 | tf_op jit(solution)/shard_map/ppermute | solution.py:135
  34.4 0.6 collective-permute-start.5
  35.0 0.5 collective-permute-start.4
  35.5 0.0 collective-permute-done.6
  35.5 3.3 %collective-permute-done.5 = bf16[40,128]{1,0:T(8,128)(2,1)S(1)} collective-permute-done((bf16[40,128]{1,0:T(8,128)(2,1)S(1)}, bf16[40,128]{1,0:T(8,128)(2,1)S(1)}, u32[]{:S(2)}, u32[]{:S(2)}) %collective-permute-start.5) | collective-permute-done | bytes 10272 | tf_op jit(solution)/shard_map/ppermute | solution.py:135
  38.8 0.2 collective-permute-done.4
  39.0 5.6 %collective-permute-start.9 = (bf16[40,128]{1,0:T(8,128)(2,1)S(1)}, bf16[40,128]{1,0:T(8,128)(2,1)S(1)}, u32[]{:S(2)}, u32[]{:S(2)}) collective-permute-start(bf16[40,128]{1,0:T(8,128)(2,1)S(1)} %add_add_fusion.1), channel_id=1, source_target_pairs={{0,192},{32,224},{64,0},{96,32},{128,64},{160,96},{192,128},{224,1... | collective-permute-start | bytes 30728 | tf_op jit(solution)/shard_map/ppermute | solution.py:135
  44.6 0.7 %collective-permute-start.8 = (bf16[40,128]{1,0:T(8,128)(2,1)S(1)}, bf16[40,128]{1,0:T(8,128)(2,1)S(1)}, u32[]{:S(2)}, u32[]{:S(2)}) collective-permute-start(bf16[40,128]{1,0:T(8,128)(2,1)S(1)} %add_add_fusion.1), channel_id=1, source_target_pairs={{0,128},{32,160},{64,192},{96,224},{128,0},{160,32},{192,64},{224,... | collective-permute-start | bytes 30728 | tf_op jit(solution)/shard_map/ppermute | solution.py:135
  45.3 2.3 %collective-permute-start.7 = (bf16[40,128]{1,0:T(8,128)(2,1)S(1)}, bf16[40,128]{1,0:T(8,128)(2,1)S(1)}, u32[]{:S(2)}, u32[]{:S(2)}) collective-permute-start(bf16[40,128]{1,0:T(8,128)(2,1)S(1)} %add_add_fusion.1), channel_id=1, source_target_pairs={{0,64},{32,96},{64,128},{96,160},{128,192},{160,224},{192,0},{224,... | collective-permute-start | bytes 30728 | tf_op jit(solution)/shard_map/ppermute | solution.py:135
  47.5 1.6 %collective-permute-done.9 = bf16[40,128]{1,0:T(8,128)(2,1)S(1)} collective-permute-done((bf16[40,128]{1,0:T(8,128)(2,1)S(1)}, bf16[40,128]{1,0:T(8,128)(2,1)S(1)}, u32[]{:S(2)}, u32[]{:S(2)}) %collective-permute-start.9) | collective-permute-done | bytes 10272 | tf_op jit(solution)/shard_map/ppermute | solution.py:135
  49.2 5.1 %collective-permute-done.8 = bf16[40,128]{1,0:T(8,128)(2,1)S(1)} collective-permute-done((bf16[40,128]{1,0:T(8,128)(2,1)S(1)}, bf16[40,128]{1,0:T(8,128)(2,1)S(1)}, u32[]{:S(2)}, u32[]{:S(2)}) %collective-permute-start.8) | collective-permute-done | bytes 10272 | tf_op jit(solution)/shard_map/ppermute | solution.py:135
  54.3 0.0 collective-permute-done.7
  54.3 1.1 %collective-permute-start.10 = (bf16[40,128]{1,0:T(8,128)(2,1)S(1)}, bf16[40,128]{1,0:T(8,128)(2,1)S(1)}, u32[]{:S(2)}, u32[]{:S(2)}) collective-permute-start(bf16[40,128]{1,0:T(8,128)(2,1)S(1)} %add_add_fusion), channel_id=1, source_target_pairs={{0,32},{32,64},{64,96},{96,128},{128,160},{160,192},{192,224},{224... | collective-permute-start | bytes 30728 | tf_op jit(solution)/shard_map/ppermute | solution.py:135
  55.4 2.8 %collective-permute-done.10 = bf16[40,128]{1,0:T(8,128)(2,1)S(1)} collective-permute-done((bf16[40,128]{1,0:T(8,128)(2,1)S(1)}, bf16[40,128]{1,0:T(8,128)(2,1)S(1)}, u32[]{:S(2)}, u32[]{:S(2)}) %collective-permute-start.10) | collective-permute-done | bytes 10272 | tf_op jit(solution)/shard_map/ppermute | solution.py:135
  58.1 0.0 copy-start
  58.1 0.0 all-to-all-done
  58.1 0.5 reshape.32.rows
  58.6 0.1 copy-done
  58.8 2.4 %select.1 = (bf16[512,1024]{1,0:T(8,128)(2,1)}, f32[1,512]{1,0:T(1,128)}, f32[4,512]{1,0:T(4,128)}) custom-call(s32[4]{0:T(128)S(1)} %copy-done, s32[1]{0:T(128)} %bitcast.base, bf16[512,1152]{1,0:T(8,128)(2,1)S(1)} %reshape.32.rows, bf16[40,128]{1,0:T(8,128)(2,1)S(1)} %add.55.side), custom_call_target="tpu_custom_call" | custom-call | tf_op jit(solution)/shard_map/select/pallas_call | solution.py:175
  (5 shorter events, 0.0 us)
Async XLA Ops:
  7.6 15.7 %copy-start.1 = (bf16[40,128]{1,0:T(8,128)(2,1)S(1)}, bf16[40,128]{1,0:T(8,128)(2,1)}, u32[]{:S(2)}) copy-start(bf16[40,128]{1,0:T(8,128)(2,1)} %get-tuple-element.9) | copy-start | bytes 30724
  7.6 50.5 %all-to-all-start = ((bf16[256,2,1152]{2,1,0:T(2,128)(2,1)}), bf16[256,2,1152]{2,1,0:T(2,128)(2,1)S(1)}, u32[]{:S(2)}, u32[]{:S(2)}) async-start(bf16[256,2,1152]{2,1,0:T(2,128)(2,1)} %reshape.31), calls=%async_computation | async-start | bytes 2359296 | tf_op jit(solution)/shard_map/all_to_all | solution.py:170
  23.3 3.1 %collective-permute-start = (bf16[40,128]{1,0:T(8,128)(2,1)S(1)}, bf16[40,128]{1,0:T(8,128)(2,1)S(1)}, u32[]{:S(2)}, u32[]{:S(2)}) collective-permute-start(bf16[40,128]{1,0:T(8,128)(2,1)S(1)} %copy-done.1), channel_id=1, source_target_pairs={{0,1},{1,0},{2,3},{3,2},{4,5},{5,4},{6,7},{7,6},{8,9},{9,8},{10,11... | collective-permute-start | bytes 30728 | tf_op jit(solution)/shard_map/ppermute | solution.py:135
  26.3 2.8 %collective-permute-start.3 = (bf16[40,128]{1,0:T(8,128)(2,1)S(1)}, bf16[40,128]{1,0:T(8,128)(2,1)S(1)}, u32[]{:S(2)}, u32[]{:S(2)}) collective-permute-start(bf16[40,128]{1,0:T(8,128)(2,1)S(1)} %add.45), channel_id=1, source_target_pairs={{0,6},{2,0},{4,2},{6,4},{1,7},{3,1},{5,3},{7,5},{8,14},{10,8},{12,... | collective-permute-start | bytes 30728 | tf_op jit(solution)/shard_map/ppermute | solution.py:135
  27.2 4.3 %collective-permute-start.2 = (bf16[40,128]{1,0:T(8,128)(2,1)S(1)}, bf16[40,128]{1,0:T(8,128)(2,1)S(1)}, u32[]{:S(2)}, u32[]{:S(2)}) collective-permute-start(bf16[40,128]{1,0:T(8,128)(2,1)S(1)} %add.45), channel_id=1, source_target_pairs={{0,4},{2,6},{4,0},{6,2},{1,5},{3,7},{5,1},{7,3},{8,12},{10,14},{12... | collective-permute-start | bytes 30728 | tf_op jit(solution)/shard_map/ppermute | solution.py:135
  27.8 4.0 %collective-permute-start.1 = (bf16[40,128]{1,0:T(8,128)(2,1)S(1)}, bf16[40,128]{1,0:T(8,128)(2,1)S(1)}, u32[]{:S(2)}, u32[]{:S(2)}) collective-permute-start(bf16[40,128]{1,0:T(8,128)(2,1)S(1)} %add.45), channel_id=1, source_target_pairs={{0,2},{2,4},{4,6},{6,0},{1,3},{3,5},{5,7},{7,1},{8,10},{10,12},{12... | collective-permute-start | bytes 30728 | tf_op jit(solution)/shard_map/ppermute | solution.py:135
  31.8 3.7 %collective-permute-start.6 = (bf16[40,128]{1,0:T(8,128)(2,1)S(1)}, bf16[40,128]{1,0:T(8,128)(2,1)S(1)}, u32[]{:S(2)}, u32[]{:S(2)}) collective-permute-start(bf16[40,128]{1,0:T(8,128)(2,1)S(1)} %add_add_fusion.2), channel_id=1, source_target_pairs={{0,24},{8,0},{16,8},{24,16},{1,25},{9,1},{17,9},{25,17},{2,26},{10... | collective-permute-start | bytes 30728 | tf_op jit(solution)/shard_map/ppermute | solution.py:135
  34.4 4.4 %collective-permute-start.5 = (bf16[40,128]{1,0:T(8,128)(2,1)S(1)}, bf16[40,128]{1,0:T(8,128)(2,1)S(1)}, u32[]{:S(2)}, u32[]{:S(2)}) collective-permute-start(bf16[40,128]{1,0:T(8,128)(2,1)S(1)} %add_add_fusion.2), channel_id=1, source_target_pairs={{0,16},{8,24},{16,0},{24,8},{1,17},{9,25},{17,1},{25,9},{2,18},{10... | collective-permute-start | bytes 30728 | tf_op jit(solution)/shard_map/ppermute | solution.py:135
  35.0 4.0 %collective-permute-start.4 = (bf16[40,128]{1,0:T(8,128)(2,1)S(1)}, bf16[40,128]{1,0:T(8,128)(2,1)S(1)}, u32[]{:S(2)}, u32[]{:S(2)}) collective-permute-start(bf16[40,128]{1,0:T(8,128)(2,1)S(1)} %add_add_fusion.2), channel_id=1, source_target_pairs={{0,8},{8,16},{16,24},{24,0},{1,9},{9,17},{17,25},{25,1},{2,10},{10... | collective-permute-start | bytes 30728 | tf_op jit(solution)/shard_map/ppermute | solution.py:135
  39.0 10.1 %collective-permute-start.9 = (bf16[40,128]{1,0:T(8,128)(2,1)S(1)}, bf16[40,128]{1,0:T(8,128)(2,1)S(1)}, u32[]{:S(2)}, u32[]{:S(2)}) collective-permute-start(bf16[40,128]{1,0:T(8,128)(2,1)S(1)} %add_add_fusion.1), channel_id=1, source_target_pairs={{0,192},{32,224},{64,0},{96,32},{128,64},{160,96},{192,128},{224,1... | collective-permute-start | bytes 30728 | tf_op jit(solution)/shard_map/ppermute | solution.py:135
  44.6 9.7 %collective-permute-start.8 = (bf16[40,128]{1,0:T(8,128)(2,1)S(1)}, bf16[40,128]{1,0:T(8,128)(2,1)S(1)}, u32[]{:S(2)}, u32[]{:S(2)}) collective-permute-start(bf16[40,128]{1,0:T(8,128)(2,1)S(1)} %add_add_fusion.1), channel_id=1, source_target_pairs={{0,128},{32,160},{64,192},{96,224},{128,0},{160,32},{192,64},{224,... | collective-permute-start | bytes 30728 | tf_op jit(solution)/shard_map/ppermute | solution.py:135
  45.3 9.0 %collective-permute-start.7 = (bf16[40,128]{1,0:T(8,128)(2,1)S(1)}, bf16[40,128]{1,0:T(8,128)(2,1)S(1)}, u32[]{:S(2)}, u32[]{:S(2)}) collective-permute-start(bf16[40,128]{1,0:T(8,128)(2,1)S(1)} %add_add_fusion.1), channel_id=1, source_target_pairs={{0,64},{32,96},{64,128},{96,160},{128,192},{160,224},{192,0},{224,... | collective-permute-start | bytes 30728 | tf_op jit(solution)/shard_map/ppermute | solution.py:135
  54.3 3.8 %collective-permute-start.10 = (bf16[40,128]{1,0:T(8,128)(2,1)S(1)}, bf16[40,128]{1,0:T(8,128)(2,1)S(1)}, u32[]{:S(2)}, u32[]{:S(2)}) collective-permute-start(bf16[40,128]{1,0:T(8,128)(2,1)S(1)} %add_add_fusion), channel_id=1, source_target_pairs={{0,32},{32,64},{64,96},{96,128},{128,160},{160,192},{192,224},{224... | collective-permute-start | bytes 30728 | tf_op jit(solution)/shard_map/ppermute | solution.py:135
  58.1 0.7 %copy-start = (s32[4]{0:T(128)S(1)}, s32[4]{0:T(128)}, u32[]{:S(2)}) copy-start(s32[4]{0:T(128)} %winners.3) | copy-start | bytes 52
